TPU v7x, 512 devices: a whole 4x4x16 slice. The times are simulated.
512 devices in a mesh: ia: 8 (over x, z_hi), ja: 8 (over z_lo), ka: 8 (over y, core).
Axes of the slice: x: 4, y: 4, z: 16 (z_hi: 2, z_lo: 8; z = z_hi * 8 + z_lo), core: 2. Of those that a mesh axis runs over, the one named last changes fastest.
Arguments:
- tensor: bfloat16 [512, 512, 2, 1024], P('ia', 'ja', None, 'ka'), may hold values from -6 to 6
- factor_two: float32 [512, 32], P('ja'), may hold values from -2 to 2
- factor_three: float32 [1024, 32], P('ka'), may hold values from -2 to 2
- factor_four: float32 [2, 32], replicated, may hold values from -2 to 2
Outputs:
- new_one: float32 [512, 32], P('ia')
- new_two: float32 [512, 32], P('ja')
All inputs are finite; a program needn't handle non-finite values.
Results may differ from a plain program's by a relative error of at most 0.0042.
Values sent between devices are 32-bit elements; how exact they have to be, the bound alone decides.
No kernel may reach another device: no remote copies, remote signals or barrier semaphores. Data moves between devices by JAX's collectives and lax.ppermute only.
A program may use at most 64 MiB of HBM per device.

v0:
```python
import jax
import jax.numpy as jnp
from jax import lax
from jax.sharding import PartitionSpec as P


def from_everyone(array, axis):
    count = lax.axis_size(axis)
    return lax.all_to_all(
        jnp.broadcast_to(array[None], (count, *array.shape)), axis, 0, 0, tiled=True
    )


def of_everyone(array, axis):
    return from_everyone(array, axis).sum(axis=0)


def gathered_total(array, axis):
    pieces = lax.all_gather(array, axis)
    return pieces.sum(axis=0)


def solve_rows(rhs, system):
    lower = jnp.linalg.cholesky(system)
    return jax.scipy.linalg.cho_solve((lower, True), rhs.T).T


def gram(factor):
    return jnp.dot(factor.T, factor, precision=lax.Precision.HIGHEST)


def along_two(root, factor):
    return jnp.einsum("abr,br->ar", root, factor, precision=lax.Precision.HIGHEST)


def along_one(root, factor):
    return jnp.einsum("abr,ar->br", root, factor, precision=lax.Precision.HIGHEST)


def per_device(tensor, factor_two, factor_three, factor_four):
    rows_first, rows_second, fourth_len, rows_third = tensor.shape
    rank_cols = factor_two.shape[1]
    khatri = (
        (factor_four[:, None, :] * factor_three[None, :, :])
        .reshape(fourth_len * rows_third, rank_cols)
        .astype(jnp.bfloat16)
    )
    local_root = jnp.dot(
        tensor.reshape(rows_first * rows_second, fourth_len * rows_third),
        khatri,
        preferred_element_type=jnp.float32,
    )
    gram_four = gram(factor_four)
    own_two = gram(factor_two)
    own_three = gram(factor_three)
    gram_two = of_everyone(own_two, "ja")
    gram_three = of_everyone(own_three, "ka")
    root = gathered_total(local_root.reshape(rows_first, rows_second * rank_cols), "ka")
    root = root.reshape(rows_first, rows_second, rank_cols)
    mode_one = of_everyone(along_two(root, factor_two), "ja")
    new_one = solve_rows(mode_one, gram_two * gram_three * gram_four)
    gram_one = of_everyone(gram(new_one), "ia")
    mode_two = of_everyone(along_one(root, new_one), "ia")
    new_two = solve_rows(mode_two, gram_one * gram_three * gram_four)
    return (new_one, new_two)


def solution(mesh):
    return jax.shard_map(
        per_device,
        mesh=mesh,
        in_specs=(P("ia", "ja", None, "ka"), P("ja", None), P("ka", None), P()),
        out_specs=(P("ia", None), P("ja", None)),
        check_vma=False,
    )
```

profile of v0, /device:TPU:1, one launch (start us, length us, event | category | flops | bytes accessed | tf_op | source)
XLA Modules:
  0.0 135.4 jit_solution(17755752463182774300)
XLA Ops:
  7.2 0.0 copy-start
  7.2 0.0 all-gather.2.cloned.1.call-start
  7.2 0.8 copy.39
  8.0 0.7 multiply_convert_fusion
  8.7 2.3 %convolution_bitcast_fusion = f32[4096,32]{0,1:T(8,128)S(1)} fusion(bf16[256,32]{1,0:T(8,128)(2,1)S(1)} %bitcast.83, bf16[512,8,2,128]{3,2,1,0:T(2,128)(2,1)} %bitcast.80), kind=kOutput, calls=%fused_computation | convolution fusion | flops 67108864 | bytes 2637824 | tf_op jit(solution)/shard_map/dot_general | solution.py:48
  11.1 0.6 copy.40
  11.7 0.0 copy-start.2
  11.7 0.0 copy-start.3
  11.7 1.8 %all_gather_reshape.3 = f32[1,64,2048]{2,1,0:T(8,128)} reshape(f32[4096,32]{1,0:T(8,128)S(1)} %copy.40) | data formatting | bytes 1048576 | tf_op jit(solution)/shard_map/all_gather;reshape | solution.py:19
  13.4 0.0 all-gather.2.cloned.1.call-update
  13.5 0.1 fusion.16
  13.7 0.7 reshape.50
  14.4 10.1 %all-to-all-start.1 = ((f32[8,1,1024]{2,1,0:T(1,128)}), f32[8,1,1024]{2,1,0:T(1,128)S(1)}, u32[]{:S(2)}, u32[]{:S(2)}) async-start(f32[8,1,1024]{2,1,0:T(1,128)} %reshape.50), calls=%async_computation.1 | async-start | bytes 65536 | tf_op jit(solution)/shard_map/all_to_all | solution.py:9
  24.4 0.1 fusion.15
  24.6 0.7 reshape.48
  25.3 3.8 %all-to-all-done.1 = f32[8,1,1024]{2,1,0:T(1,128)S(1)} async-done(((f32[8,1,1024]{2,1,0:T(1,128)}), f32[8,1,1024]{2,1,0:T(1,128)S(1)}, u32[]{:S(2)}, u32[]{:S(2)}) %all-to-all-start.1) | async-done | bytes 32800 | tf_op jit(solution)/shard_map/all_to_all | solution.py:9
  29.2 8.1 %all-to-all-start = ((f32[8,1,1024]{2,1,0:T(1,128)}), f32[8,1,1024]{2,1,0:T(1,128)S(1)}, u32[]{:S(2)}, u32[]{:S(2)}) async-start(f32[8,1,1024]{2,1,0:T(1,128)} %reshape.48), calls=%async_computation | async-start | bytes 65536 | tf_op jit(solution)/shard_map/all_to_all | solution.py:9
  37.3 0.5 broadcast.63
  37.8 0.7 reduce.6
  38.5 0.1 reshape.51
  38.7 0.1 copy.36
  38.7 8.1 %all-to-all-done = f32[8,1,1024]{2,1,0:T(1,128)S(1)} async-done(((f32[8,1,1024]{2,1,0:T(1,128)}), f32[8,1,1024]{2,1,0:T(1,128)S(1)}, u32[]{:S(2)}, u32[]{:S(2)}) %all-to-all-start) | async-done | bytes 32800 | tf_op jit(solution)/shard_map/all_to_all | solution.py:9
  46.8 0.7 reduce.5
  47.5 0.1 reshape.49
  47.6 0.1 copy.35
  47.7 0.2 multiply_multiply_fusion.1
  47.9 0.1 copy.38
  48.0 2.9 %cholesky.44 = f32[32,32]{1,0:T(8,128)S(1)} custom-call(f32[32,32]{1,0:T(8,128)S(1)} %fusion.14), custom_call_target="Cholesky" | custom-call | tf_op jit(solution)/shard_map/jit(cholesky)/cholesky | solution.py:24
  51.0 8.1 %all-gather.2.cloned.1.call-done = f32[8,64,2048]{2,1,0:T(8,128)} async-done(((f32[1,64,2048]{2,1,0:T(8,128)}), f32[8,64,2048]{2,1,0:T(8,128)}) %all-gather.2.cloned.1.call-update) | async-done | bytes 4194320 | tf_op jit(solution)/shard_map/all_gather | solution.py:19
  59.1 2.5 %reduce_sum.56 = f32[64,2048]{1,0:T(8,128)S(1)} reduce(f32[8,64,2048]{2,1,0:T(8,128)} %all-gather.2.cloned.1.call-done, f32[]{:T(128)} %constant.36.clone.1), dimensions={0}, to_apply=%region_4.6 | reduce | flops 917504 | bytes 4718596 | tf_op jit(solution)/shard_map/reduce_sum | solution.py:20
  61.5 0.3 copy.41
  61.9 0.6 copy.47
  62.5 1.7 %fusion.17 = f32[32,1,64]{2,1,0:T(1,128)S(1)} fusion(f32[64,64,32]{1,0,2:T(8,128)S(1)} %copy.47, f32[64,32,1]{0,2,1:T(1,128)S(1)} %bitcast.78), kind=kOutput, calls=%fused_computation.36 | convolution fusion | flops 1572864 | bytes 540672 | tf_op jit(solution)/shard_map/abr,br->ar/dot_general | solution.py:33
  64.3 0.7 reshape.46
  65.0 9.7 %all-to-all-start.2 = ((f32[8,1,2048]{2,1,0:T(1,128)}), f32[8,1,2048]{2,1,0:T(1,128)S(1)}, u32[]{:S(2)}, u32[]{:S(2)}) async-start(f32[8,1,2048]{2,1,0:T(1,128)} %reshape.46), calls=%async_computation.2 | async-start | bytes 131072 | tf_op jit(solution)/shard_map/all_to_all | solution.py:9
  74.8 0.6 compare_reduce_fusion.1
  75.4 0.7 fusion.2
  76.0 2.4 %custom-call.8 = f32[1,32,32]{1,2,0:T(8,128)S(1)} custom-call(f32[1,32,32]{2,1,0:T(8,128)S(1)} %fusion.2), custom_call_target="InvertDiagBlocksLowerTriangular" | custom-call | tf_op jit(solution)/shard_map/jit(_cho_solve)/triangular_solve | solution.py:25
  78.5 6.1 %all-to-all-done.2 = f32[8,1,2048]{2,1,0:T(1,128)S(1)} async-done(((f32[8,1,2048]{2,1,0:T(1,128)}), f32[8,1,2048]{2,1,0:T(1,128)S(1)}, u32[]{:S(2)}, u32[]{:S(2)}) %all-to-all-start.2) | async-done | bytes 65568 | tf_op jit(solution)/shard_map/all_to_all | solution.py:9
  84.5 0.8 reduce.4
  85.4 0.1 reshape.47
  85.5 0.2 fusion.9
  85.7 0.1 fusion.11
  85.8 0.0 copy-start.1
  85.8 0.1 fusion.18
  86.0 1.0 fusion.19
  87.0 0.7 reshape.54
  87.7 7.9 %all-to-all-start.3 = ((f32[8,1,1024]{2,1,0:T(1,128)}), f32[8,1,1024]{2,1,0:T(1,128)S(1)}, u32[]{:S(2)}, u32[]{:S(2)}) async-start(f32[8,1,1024]{2,1,0:T(1,128)} %reshape.54), calls=%async_computation.3 | async-start | bytes 65536 | tf_op jit(solution)/shard_map/all_to_all | solution.py:9
  95.6 0.7 reshape.52
  96.4 13.1 %all-to-all-done.3 = f32[8,1,1024]{2,1,0:T(1,128)S(1)} async-done(((f32[8,1,1024]{2,1,0:T(1,128)}), f32[8,1,1024]{2,1,0:T(1,128)S(1)}, u32[]{:S(2)}, u32[]{:S(2)}) %all-to-all-start.3) | async-done | bytes 32800 | tf_op jit(solution)/shard_map/all_to_all | solution.py:9
  109.4 3.3 %all-to-all-start.4 = ((f32[8,1,2048]{2,1,0:T(1,128)}), f32[8,1,2048]{2,1,0:T(1,128)S(1)}, u32[]{:S(2)}, u32[]{:S(2)}) async-start(f32[8,1,2048]{2,1,0:T(1,128)} %reshape.52), calls=%async_computation.4 | async-start | bytes 131072 | tf_op jit(solution)/shard_map/all_to_all | solution.py:9
  112.8 0.7 reduce.8
  113.5 0.1 reshape.55
  113.6 0.1 copy.42
  113.7 0.1 copy.45
  113.8 2.9 %cholesky.55 = f32[32,32]{1,0:T(8,128)S(1)} custom-call(f32[32,32]{1,0:T(8,128)S(1)} %fusion.8), custom_call_target="Cholesky" | custom-call | tf_op jit(solution)/shard_map/jit(cholesky)/cholesky | solution.py:24
  116.8 0.7 compare_reduce_fusion
  117.4 0.6 fusion.3
  118.1 2.4 %custom-call.9 = f32[1,32,32]{1,2,0:T(8,128)S(1)} custom-call(f32[1,32,32]{2,1,0:T(8,128)S(1)} %fusion.3), custom_call_target="InvertDiagBlocksLowerTriangular" | custom-call | tf_op jit(solution)/shard_map/jit(_cho_solve)/triangular_solve | solution.py:25
  120.5 6.1 %all-to-all-done.4 = f32[8,1,2048]{2,1,0:T(1,128)S(1)} async-done(((f32[8,1,2048]{2,1,0:T(1,128)}), f32[8,1,2048]{2,1,0:T(1,128)S(1)}, u32[]{:S(2)}, u32[]{:S(2)}) %all-to-all-start.4) | async-done | bytes 65568 | tf_op jit(solution)/shard_map/all_to_all | solution.py:9
  126.6 0.8 reduce.7
  127.4 0.1 reshape.53
  127.5 0.2 fusion.4
  127.8 0.8 convolution_bitcast_fusion.1
  (19 shorter events, 0.2 us)
Async XLA Ops:
  7.2 17.3 %copy-start = (f32[64,32]{0,1:T(8,128)S(1)}, f32[64,32]{0,1:T(8,128)}, u32[]{:S(2)}) copy-start(f32[64,32]{0,1:T(8,128)} %param.8) | copy-start | bytes 24580
  7.2 51.9 %all-gather.2.cloned.1.call-start = ((), (), s32[]{:S(2)}) async-start(), calls=%async_computation.5 | async-start | bytes 4718592 | tf_op jit(solution)/shard_map/all_gather | solution.py:19
  11.7 1.8 %copy-start.2 = (f32[128,32]{0,1:T(8,128)S(1)}, f32[128,32]{0,1:T(8,128)}, u32[]{:S(2)}) copy-start(f32[128,32]{0,1:T(8,128)} %param.9) | copy-start | bytes 49156
  11.7 36.0 %copy-start.3 = (f32[2,32]{1,0:T(2,128)S(1)}, f32[2,32]{1,0:T(2,128)}, u32[]{:S(2)}) copy-start(f32[2,32]{1,0:T(2,128)} %param.10) | copy-start | bytes 772
  14.4 14.8 %all-to-all-start.1 = ((f32[8,1,1024]{2,1,0:T(1,128)}), f32[8,1,1024]{2,1,0:T(1,128)S(1)}, u32[]{:S(2)}, u32[]{:S(2)}) async-start(f32[8,1,1024]{2,1,0:T(1,128)} %reshape.50), calls=%async_computation.1 | async-start | bytes 65536 | tf_op jit(solution)/shard_map/all_to_all | solution.py:9
  29.2 17.6 %all-to-all-start = ((f32[8,1,1024]{2,1,0:T(1,128)}), f32[8,1,1024]{2,1,0:T(1,128)S(1)}, u32[]{:S(2)}, u32[]{:S(2)}) async-start(f32[8,1,1024]{2,1,0:T(1,128)} %reshape.48), calls=%async_computation | async-start | bytes 65536 | tf_op jit(solution)/shard_map/all_to_all | solution.py:9
  65.0 19.5 %all-to-all-start.2 = ((f32[8,1,2048]{2,1,0:T(1,128)}), f32[8,1,2048]{2,1,0:T(1,128)S(1)}, u32[]{:S(2)}, u32[]{:S(2)}) async-start(f32[8,1,2048]{2,1,0:T(1,128)} %reshape.46), calls=%async_computation.2 | async-start | bytes 131072 | tf_op jit(solution)/shard_map/all_to_all | solution.py:9
  85.8 42.7 %copy-start.1 = (f32[32,64]{1,0:T(8,128)}, f32[32,64]{1,0:T(8,128)S(1)}, u32[]{:S(2)}) copy-start(f32[32,64]{1,0:T(8,128)S(1)} %fusion.11) | copy-start | bytes 24580
  87.7 21.8 %all-to-all-start.3 = ((f32[8,1,1024]{2,1,0:T(1,128)}), f32[8,1,1024]{2,1,0:T(1,128)S(1)}, u32[]{:S(2)}, u32[]{:S(2)}) async-start(f32[8,1,1024]{2,1,0:T(1,128)} %reshape.54), calls=%async_computation.3 | async-start | bytes 65536 | tf_op jit(solution)/shard_map/all_to_all | solution.py:9
  109.4 17.2 %all-to-all-start.4 = ((f32[8,1,2048]{2,1,0:T(1,128)}), f32[8,1,2048]{2,1,0:T(1,128)S(1)}, u32[]{:S(2)}, u32[]{:S(2)}) async-start(f32[8,1,2048]{2,1,0:T(1,128)} %reshape.52), calls=%async_computation.4 | async-start | bytes 131072 | tf_op jit(solution)/shard_map/all_to_all | solution.py:9
Sparse Core Ops, SparseCore 0:
  13.6 45.4 all-gather.1
where the time goes:
time: 138 us; the launch traced here: 135 us
  waiting for transfers between devices  45.3 us (33%)
  starting transfers between devices  39.2 us (28%)
  other arithmetic  20.4 us (15%)
  between operations  14.3 us (10%)
  local copies, waits for them, and re-layouts  9.2 us (7%)
  matrix products  6.96 us (5%)
    all_to_all x5, starting transfers between devices, from_everyone(): lax.all_to_all(jnp.broadcast_to(array[None], (count, *array.shape)), axis...  39.2 us
    all_to_all x5, waiting for transfers between devices, from_everyone(): lax.all_to_all(jnp.broadcast_to(array[None], (count, *array.shape)), axis...  37.2 us
    all_gather x1, waiting for transfers between devices, gathered_total(): pieces = lax.all_gather(array, axis)  8.1 us
    another operation x6, other arithmetic, solve_rows(): lower = jnp.linalg.cholesky(system)  7.21 us
    another operation x4, other arithmetic, solve_rows(): return jax.scipy.linalg.cho_solve((lower, True), rhs.T).T  6.13 us
    unnamed x21, local copies, waits for them, and re-layouts  4.98 us
    all_to_all x5, other arithmetic, from_everyone(): lax.all_to_all(jnp.broadcast_to(array[None], (count, *array.shape)), axis...  3.75 us
  transfers between devices with their start and end apart: 6, of which 6 were waited for; matrix products, arithmetic and copies ran while one was open for 14% of the time, Pallas kernels for 0%

commit v1 on v0

v1 whole, which is shorter than its diff:
```python
import functools

import jax
import jax.numpy as jnp
from jax import lax
from jax.experimental import pallas as pl
from jax.experimental.pallas import tpu as pltpu
from jax.sharding import PartitionSpec as P

HI = lax.Precision.HIGHEST
LANES = 128
SUB = 8
VMEM = pl.BlockSpec(memory_space=pltpu.VMEM)
PARAMS = pltpu.CompilerParams(vmem_limit_bytes=24 * 1024 * 1024)


def iota(shape, dim):
    return lax.broadcasted_iota(jnp.int32, shape, dim)


def contract_last(a, b, precision=HI):
    return lax.dot_general(
        a, b, (((1,), (1,)), ((), ())), precision=precision, preferred_element_type=jnp.float32
    )


def fold_matrix(rank, fourth):
    shape = (rank, fourth * rank)
    return (iota(shape, 1) % rank == iota(shape, 0)).astype(jnp.float32)


def fill_slots(out_ref, value):
    for slot in range(out_ref.shape[0]):
        out_ref[slot] = value


def summed_slots(ref):
    parts = [ref[s] for s in range(ref.shape[0])]
    while len(parts) > 1:
        parts = [a + b for a, b in zip(parts[::2], parts[1::2])]
    return parts[0]


def root_kernel(first, chunks, x_hbm, f2t_ref, f3t_ref, f4_ref, prod_ref, pay_ref, x_ref, r_ref, sems):
    fourth, rank = f4_ref.shape
    second = f2t_ref.shape[1]
    wide = fourth * rank
    rows = second * fourth
    per = first // chunks
    span = per * rows

    def fetch(c):
        part = pl.ds(c * span, span)
        return pltpu.make_async_copy(x_hbm.at[part], x_ref.at[part], sems.at[c])

    for c in range(chunks):
        fetch(c).start()

    f2t = f2t_ref[...]
    f3t = f3t_ref[...]
    f4 = f4_ref[...]
    eye = iota((rank, rank), 0) == iota((rank, rank), 1)
    cols = [
        jnp.sum(jnp.where(eye, f4[l : l + 1, :], 0.0), axis=1, keepdims=True) for l in range(fourth)
    ]
    kt = jnp.concatenate([c * f3t for c in cols], axis=0).astype(jnp.bfloat16)

    gram_four = sum(cols[l] * f4[l : l + 1, :] for l in range(fourth))
    gram_two = contract_last(f2t, f2t)
    gram_rest = contract_last(f3t, f3t) * gram_four
    grams = jnp.concatenate(
        [jnp.zeros((rank, LANES - 2 * rank), jnp.float32), gram_two, gram_rest * 0.125], axis=1
    )

    spread = (iota((rows, second), 0) // fourth == iota((rows, second), 1)).astype(jnp.float32)
    weight = contract_last(spread, jnp.concatenate([f2t] * fourth, axis=0))
    keep = iota((rows, wide), 0) % fourth == iota((rows, wide), 1) // rank
    weight = jnp.where(keep, weight, 0.0).reshape(1, rows // SUB, SUB, wide)

    for c in range(chunks):
        fetch(c).wait()
        part = contract_last(x_ref[pl.ds(c * span, span), :], kt, None)
        prod_ref[pl.ds(c * span, span), :] = part
        r_ref[pl.ds(c * per * SUB, per * SUB), :] = jnp.sum(
            part.reshape(per, rows // SUB, SUB, wide) * weight, axis=1
        ).reshape(per * SUB, wide)

    total = r_ref[pl.ds(0, first, stride=SUB), :]
    for s in range(1, SUB):
        total = total + r_ref[pl.ds(s, first, stride=SUB), :]
    mode_one = contract_last(fold_matrix(rank, fourth), total)
    mode_one = jnp.concatenate(
        [mode_one, jnp.zeros((rank, LANES - first), jnp.float32)], axis=1
    )
    fill_slots(pay_ref, mode_one + grams)


def relay_kernel(lo, hi, in_ref, out_ref):
    value = summed_slots(in_ref)
    lane = iota(value.shape, 1)
    fill_slots(out_ref, jnp.where((lane >= lo) & (lane < hi), value * 0.125, value))


def eliminate(tiles, start, rank):
    lanes = tiles[0].shape[1]
    count = rank // SUB
    row = iota((SUB, lanes), 0)
    for b in range(count):
        cols = [
            [
                jnp.broadcast_to(tiles[t][:, start + b * SUB + c : start + b * SUB + c + 1], (SUB, lanes))
                for c in range(SUB)
            ]
            for t in range(count)
        ]
        own = tiles[b]
        piv = cols[b]
        for c in range(SUB):
            factor = piv[c]
            inverse = 1.0 / factor[c : c + 1, :]
            lead = own[c : c + 1, :] * inverse
            here = row == c
            own = jnp.where(here, lead, own - factor * lead)
            for d in range(c + 1, SUB):
                lead_d = piv[d][c : c + 1, :] * inverse
                piv[d] = jnp.where(here, lead_d, piv[d] - factor * lead_d)
        tiles[b] = own
        for t in range(count):
            if t != b:
                acc = tiles[t]
                for c in range(SUB):
                    acc = acc - cols[t][c] * own[c : c + 1, :]
                tiles[t] = acc
    return tiles


def solved(value, rank):
    lanes = value.shape[1]
    start = lanes - 2 * rank
    system = value * pltpu.roll(value, lanes - rank, 1)
    lane = iota(value.shape, 1)
    aug = jnp.where(lane < start, value, system)
    tiles = [aug[t * SUB : (t + 1) * SUB, :] for t in range(rank // SUB)]
    return jnp.concatenate(eliminate(tiles, start, rank), axis=0)


def middle_kernel(first, second, fourth, in_ref, prod_ref, new_ref, pay_ref, nx_ref, acc_ref):
    value = summed_slots(in_ref)
    rank, lanes = value.shape
    wide = fourth * rank
    rows = second * fourth
    start = lanes - 2 * rank
    answer = solved(value, rank)[:, :first]
    new_ref[...] = answer
    flat = jnp.transpose(answer)
    nx_ref[...] = jnp.concatenate([flat] * fourth, axis=1)

    def step(i, acc):
        at = pl.multiple_of(i * rows, rows)
        return acc + prod_ref[pl.ds(at, rows), :] * nx_ref[pl.ds(i, 1), :]

    acc_ref[...] = lax.fori_loop(
        0, first, step, jnp.zeros((rows, wide), jnp.float32), unroll=8
    )
    half = iota((second, wide), 1) // rank
    picked = acc_ref[pl.ds(0, second, stride=fourth), :]
    for l in range(1, fourth):
        picked = jnp.where(half == l, acc_ref[pl.ds(l, second, stride=fourth), :], picked)
    mode_two = contract_last(fold_matrix(rank, fourth), picked)
    gram_one = contract_last(answer, answer)
    head = jnp.concatenate(
        [mode_two, gram_one, jnp.zeros((rank, rank), jnp.float32)], axis=1
    )
    lane = iota(value.shape, 1)
    fill_slots(pay_ref, jnp.where(lane >= start + rank, value * 0.125, head))


def last_kernel(second, in_ref, new_ref):
    value = summed_slots(in_ref)
    new_ref[...] = solved(value, value.shape[0])[:, :second]


def exchanged(array, axis):
    return lax.all_to_all(array, axis, 0, 0, tiled=True)


def per_device(tensor, factor_two, factor_three, factor_four):
    first, second, fourth, third = tensor.shape
    rank = factor_two.shape[1]
    wide = fourth * rank
    rows = first * second * fourth
    chunks = 8
    pay = jax.ShapeDtypeStruct((8, rank, LANES), jnp.float32)
    prod, sent = pl.pallas_call(
        functools.partial(root_kernel, first, chunks),
        out_shape=(jax.ShapeDtypeStruct((rows, wide), jnp.float32), pay),
        in_specs=[pl.BlockSpec(memory_space=pl.ANY), VMEM, VMEM, VMEM],
        out_specs=(VMEM, VMEM),
        scratch_shapes=[
            pltpu.VMEM((rows, third), jnp.bfloat16),
            pltpu.VMEM((first * SUB, wide), jnp.float32),
            pltpu.SemaphoreType.DMA((chunks,)),
        ],
        compiler_params=PARAMS,
        name="root",
    )(tensor.reshape(rows, third), factor_two.T, factor_three.T, factor_four)

    def relay(array, lo, hi):
        return pl.pallas_call(
            functools.partial(relay_kernel, lo, hi),
            out_shape=pay,
            in_specs=[VMEM],
            out_specs=VMEM,
            compiler_params=PARAMS,
            name="relay",
        )(array)

    start = LANES - 2 * rank
    got = exchanged(sent, "ja")
    got = exchanged(relay(got, start, start + rank), "ka")
    new_one, sent = pl.pallas_call(
        functools.partial(middle_kernel, first, second, fourth),
        out_shape=(jax.ShapeDtypeStruct((rank, first), jnp.float32), pay),
        in_specs=[VMEM, VMEM],
        out_specs=(VMEM, VMEM),
        scratch_shapes=[
            pltpu.VMEM((first, wide), jnp.float32),
            pltpu.VMEM((second * fourth, wide), jnp.float32),
        ],
        compiler_params=PARAMS,
        name="middle",
    )(got, prod)
    got = exchanged(sent, "ia")
    got = exchanged(relay(got, start, LANES), "ka")
    new_two = pl.pallas_call(
        functools.partial(last_kernel, second),
        out_shape=jax.ShapeDtypeStruct((rank, second), jnp.float32),
        in_specs=[VMEM],
        out_specs=VMEM,
        compiler_params=PARAMS,
        name="last",
    )(got)
    return (new_one.T, new_two.T)


def solution(mesh):
    return jax.shard_map(
        per_device,
        mesh=mesh,
        in_specs=(P("ia", "ja", None, "ka"), P("ja", None), P("ka", None), P()),
        out_specs=(P("ia", None), P("ja", None)),
        check_vma=False,
    )
```

time: 138 us -> 81.6 us (0.59)
  the two profiles are of different devices: /device:TPU:1 before, /device:TPU:32 now
where the time goes in v1:
time: 81.6 us; the launch traced here: 81.1 us
  blocking collectives  70.2 us (86%)
  Pallas kernels  6.52 us (8%)
  local copies, waits for them, and re-layouts  3.7 us (5%)
    all_to_all x4, blocking collectives, exchanged(): return lax.all_to_all(array, axis, 0, 0, tiled=True)  70.2 us
    unnamed x8, local copies, waits for them, and re-layouts  3.7 us
    pallas_call x1, Pallas kernels, per_device(): pl.pallas_call(functools.partial(root_kernel, first, chunks), out_shape=(...  2.87 us
    pallas_call x1, Pallas kernels, per_device(): pl.pallas_call(functools.partial(middle_kernel, first, second, fourth), o...  2.02 us

profile of v1, /device:TPU:32, one launch (start us, length us, event | category | flops | bytes accessed | tf_op | source)
XLA Modules:
  0.0 81.1 jit_solution(14120152909480849488)
XLA Ops:
  0.6 0.0 copy-start
  0.6 1.6 %copy-done = bf16[64,64,2,128]{3,2,1,0:T(2,128)(2,1)S(1)} copy-done((bf16[64,64,2,128]{3,2,1,0:T(2,128)(2,1)S(1)}, bf16[64,64,2,128]{3,2,1,0:T(2,128)(2,1)}, u32[]{:S(2)}) %copy-start) | copy-done | bytes 2097176
  2.2 0.0 copy-start.1
  2.2 0.7 copy-done.1
  2.9 0.0 copy-start.2
  2.9 0.7 copy-done.2
  3.7 0.0 copy-start.3
  3.7 0.7 copy-done.3
  4.3 2.9 %root.1 = (f32[8192,64]{1,0:T(8,128)S(1)}, f32[8,32,128]{2,1,0:T(8,128)S(1)}) custom-call(bf16[8192,128]{1,0:T(8,128)(2,1)S(1)} %bitcast.5, f32[32,64]{1,0:T(8,128)S(1)} %bitcast.6, f32[32,128]{1,0:T(8,128)S(1)} %bitcast.7, f32[2,32]{1,0:T(2,128)S(1)} %copy-done.3), custom_call_target="tpu_custom_call" | custom-call | tf_op jit(solution)/shard_map/root/pallas_call | solution.py:194
  7.2 23.6 %all_to_all.20.in_ref = f32[8,32,128]{2,1,0:T(8,128)S(1)} all-to-all(f32[8,32,128]{2,1,0:T(8,128)S(1)} %get-tuple-element.6), channel_id=1, replica_groups=mesh['ia'=8,'ja'=8,'ka'=8] {'ja'}, dimensions={0} | all-to-all | bytes 262144 | tf_op jit(solution)/shard_map/all_to_all | solution.py:184
  30.8 10.4 %all_to_all.21.in_ref = f32[8,32,128]{2,1,0:T(8,128)S(1)} all-to-all(f32[8,32,128]{2,1,0:T(8,128)S(1)} %relay.2), channel_id=1, replica_groups=mesh['ia'=8,'ja'=8,'ka'=8] {'ka'}, dimensions={0} | all-to-all | bytes 262144 | tf_op jit(solution)/shard_map/all_to_all | solution.py:184
  41.2 2.0 %middle.1 = (f32[32,64]{1,0:T(8,128)}, f32[8,32,128]{2,1,0:T(8,128)S(1)}) custom-call(f32[8,32,128]{2,1,0:T(8,128)S(1)} %all_to_all.21.in_ref, f32[8192,64]{1,0:T(8,128)S(1)} %get-tuple-element.7.prod_ref), custom_call_target="tpu_custom_call" | custom-call | tf_op jit(solution)/shard_map/middle/pallas_call | solution.py:221
  43.2 27.8 %all_to_all.22.in_ref = f32[8,32,128]{2,1,0:T(8,128)S(1)} all-to-all(f32[8,32,128]{2,1,0:T(8,128)S(1)} %get-tuple-element.9), channel_id=1, replica_groups=mesh['ia'=8,'ja'=8,'ka'=8] {'ia'}, dimensions={0} | all-to-all | bytes 262144 | tf_op jit(solution)/shard_map/all_to_all | solution.py:184
  71.0 8.5 %all_to_all.23.in_ref = f32[8,32,128]{2,1,0:T(8,128)S(1)} all-to-all(f32[8,32,128]{2,1,0:T(8,128)S(1)} %relay.3), channel_id=1, replica_groups=mesh['ia'=8,'ja'=8,'ka'=8] {'ka'}, dimensions={0} | all-to-all | bytes 262144 | tf_op jit(solution)/shard_map/all_to_all | solution.py:184
  79.5 1.6 %last.1 = f32[32,64]{1,0:T(8,128)} custom-call(f32[8,32,128]{2,1,0:T(8,128)S(1)} %all_to_all.23.in_ref), custom_call_target="tpu_custom_call" | custom-call | tf_op jit(solution)/shard_map/last/pallas_call | solution.py:235
  (2 shorter events, 0.0 us)
Async XLA Ops:
  0.6 1.6 %copy-start = (bf16[64,64,2,128]{3,2,1,0:T(2,128)(2,1)S(1)}, bf16[64,64,2,128]{3,2,1,0:T(2,128)(2,1)}, u32[]{:S(2)}) copy-start(bf16[64,64,2,128]{3,2,1,0:T(2,128)(2,1)} %param.4) | copy-start | bytes 6291460
  2.2 0.7 copy-start.1
  2.9 0.7 copy-start.2
  3.7 0.7 copy-start.3

commit v2 on v1

v2 whole, which is shorter than its diff:
```python
import functools

import jax
import jax.numpy as jnp
from jax import lax
from jax.experimental import pallas as pl
from jax.experimental.pallas import tpu as pltpu
from jax.sharding import PartitionSpec as P

HI = lax.Precision.HIGHEST
LANES = 128
SUB = 8
PACK = 16
VMEM = pl.BlockSpec(memory_space=pltpu.VMEM)
HBM = pl.BlockSpec(memory_space=pltpu.HBM)
PARAMS = pltpu.CompilerParams(vmem_limit_bytes=24 * 1024 * 1024)


def iota(shape, dim):
    return lax.broadcasted_iota(jnp.int32, shape, dim)


def contract_last(a, b, precision=HI):
    return lax.dot_general(
        a, b, (((1,), (1,)), ((), ())), precision=precision, preferred_element_type=jnp.float32
    )


def fold_matrix(rank, fourth):
    shape = (rank, fourth * rank)
    return (iota(shape, 1) % rank == iota(shape, 0)).astype(jnp.float32)


def fill_slots(out_ref, value, at=0):
    for slot in range(out_ref.shape[0]):
        out_ref[slot, at : at + value.shape[0], :] = value


def summed_slots(ref, lo, hi):
    parts = [ref[s, lo:hi, :] for s in range(ref.shape[0])]
    while len(parts) > 1:
        parts = [a + b for a, b in zip(parts[::2], parts[1::2])]
    return parts[0]


def packed(array, groups):
    rows = array.shape[0] // groups
    return jnp.concatenate([array[g * rows : (g + 1) * rows, :] for g in range(groups)], axis=1)


def root_kernel(
    first, chunks, x_hbm, f2t_hbm, f3t_hbm, f4_hbm, prod_ref, pay_ref, rest_ref,
    x_ref, f2t_ref, f3t_ref, f4_ref, r_ref, sems,
):
    fourth, rank = f4_ref.shape
    second = f2t_ref.shape[1]
    wide = fourth * rank
    rows = second * fourth
    per = first // chunks
    span = per * rows

    def fetch(c):
        part = pl.ds(c * span, span)
        return pltpu.make_async_copy(x_hbm.at[part], x_ref.at[part], sems.at[c])

    small = [
        pltpu.make_async_copy(src, dst, sems.at[chunks + n])
        for n, (src, dst) in enumerate(((f4_hbm, f4_ref), (f3t_hbm, f3t_ref), (f2t_hbm, f2t_ref)))
    ]
    for copy in small:
        copy.start()
    for c in range(chunks):
        fetch(c).start()
    for copy in small:
        copy.wait()

    f2t = f2t_ref[...]
    f3t = f3t_ref[...]
    f4 = f4_ref[...]
    eye = iota((rank, rank), 0) == iota((rank, rank), 1)
    cols = [
        jnp.sum(jnp.where(eye, f4[l : l + 1, :], 0.0), axis=1, keepdims=True) for l in range(fourth)
    ]
    kt = jnp.concatenate([c * f3t for c in cols], axis=0).astype(jnp.bfloat16)

    spread = (iota((rows, second), 0) // fourth == iota((rows, second), 1)).astype(jnp.float32)
    weight = contract_last(spread, jnp.concatenate([f2t] * fourth, axis=0))
    keep = iota((rows, wide), 0) % fourth == iota((rows, wide), 1) // rank
    weight = jnp.where(keep, weight, 0.0).reshape(1, rows // SUB, SUB, wide)

    gram_four = sum(cols[l] * f4[l : l + 1, :] for l in range(fourth))
    groups = rank // SUB
    fill_slots(pay_ref, packed(contract_last(f2t, f2t), groups), PACK)
    rest_ref[...] = packed(contract_last(f3t, f3t) * gram_four, groups)

    for c in range(chunks):
        fetch(c).wait()
        part = contract_last(x_ref[pl.ds(c * span, span), :], kt, None)
        prod_ref[pl.ds(c * span, span), :] = part
        r_ref[pl.ds(c * per * SUB, per * SUB), :] = jnp.sum(
            part.reshape(per, rows // SUB, SUB, wide) * weight, axis=1
        ).reshape(per * SUB, wide)

    total = r_ref[pl.ds(0, first, stride=SUB), :]
    for s in range(1, SUB):
        total = total + r_ref[pl.ds(s, first, stride=SUB), :]
    fill_slots(pay_ref, packed(contract_last(fold_matrix(rank, fourth), total), 2))


def relay_kernel(in_ref, rest_ref, out_ref):
    fill_slots(out_ref, summed_slots(in_ref, 0, PACK))
    fill_slots(out_ref, rest_ref[...], PACK)


def relay_short_kernel(in_ref, out_ref):
    fill_slots(out_ref, summed_slots(in_ref, 0, PACK))


def eliminate(tiles, start, rank):
    lanes = tiles[0].shape[1]
    count = rank // SUB
    row = iota((SUB, lanes), 0)
    for b in range(count):
        cols = [
            [
                jnp.broadcast_to(tiles[t][:, start + b * SUB + c : start + b * SUB + c + 1], (SUB, lanes))
                for c in range(SUB)
            ]
            for t in range(count)
        ]
        own = tiles[b]
        piv = cols[b]
        for c in range(SUB):
            factor = piv[c]
            inverse = 1.0 / factor[c : c + 1, :]
            lead = own[c : c + 1, :] * inverse
            here = row == c
            own = jnp.where(here, lead, own - factor * lead)
            for d in range(c + 1, SUB):
                lead_d = piv[d][c : c + 1, :] * inverse
                piv[d] = jnp.where(here, lead_d, piv[d] - factor * lead_d)
        tiles[b] = own
        for t in range(count):
            if t != b:
                acc = tiles[t]
                for c in range(SUB):
                    acc = acc - cols[t][c] * own[c : c + 1, :]
                tiles[t] = acc
    return tiles


def solved(rhs, gram, rank):
    lanes = rhs.shape[1]
    start = lanes // 2
    lane = iota((SUB, lanes), 1)
    half = rhs.shape[0] // SUB
    other = pltpu.roll(rhs, start, 1)
    tiles = []
    for t in range(rank // SUB):
        own = (rhs if t < half else other)[(t % half) * SUB : (t % half + 1) * SUB, :]
        shift = (start - t * rank) % lanes
        system = pltpu.roll(gram, shift, 1) if shift else gram
        tiles.append(jnp.where(lane < start, own, system))
    return jnp.concatenate(eliminate(tiles, start, rank), axis=0)


def middle_kernel(
    first, second, fourth, two_ref, in_ref, prod_ref, new_hbm, pay_ref, rest_ref,
    new_ref, nx_ref, acc_ref, sem,
):
    rank = new_ref.shape[0]
    wide = fourth * rank
    rows = second * fourth
    rest = summed_slots(in_ref, PACK, PACK + SUB)
    gram_two = summed_slots(two_ref, PACK, PACK + SUB)
    rest_ref[...] = rest
    answer = solved(summed_slots(in_ref, 0, PACK), gram_two * rest, rank)[:, :first]
    new_ref[...] = answer
    leave = pltpu.make_async_copy(new_ref, new_hbm, sem)
    leave.start()
    flat = jnp.transpose(answer)
    nx_ref[...] = jnp.concatenate([flat] * fourth, axis=1)
    fill_slots(pay_ref, packed(contract_last(answer, answer), rank // SUB), PACK)

    def step(i, acc):
        at = pl.multiple_of(i * rows, rows)
        return acc + prod_ref[pl.ds(at, rows), :] * nx_ref[pl.ds(i, 1), :]

    acc_ref[...] = lax.fori_loop(
        0, first, step, jnp.zeros((rows, wide), jnp.float32), unroll=8
    )
    half = iota((second, wide), 1) // rank
    picked = acc_ref[pl.ds(0, second, stride=fourth), :]
    for l in range(1, fourth):
        picked = jnp.where(half == l, acc_ref[pl.ds(l, second, stride=fourth), :], picked)
    fill_slots(pay_ref, packed(contract_last(fold_matrix(rank, fourth), picked), 2))
    leave.wait()


def last_kernel(second, one_ref, rest_ref, in_ref, new_ref):
    gram_one = summed_slots(one_ref, PACK, PACK + SUB)
    rhs = summed_slots(in_ref, 0, PACK)
    new_ref[...] = solved(rhs, gram_one * rest_ref[...], new_ref.shape[0])[:, :second]


def held(array):
    return pltpu.with_memory_space_constraint(array, pltpu.HBM)


def exchanged(array, axis):
    return lax.all_to_all(array, axis, 0, 0, tiled=True)


def call(kernel, name, outs, ins, scratch=()):
    return pl.pallas_call(
        kernel,
        out_shape=tuple(jax.ShapeDtypeStruct(shape, jnp.float32) for shape, _ in outs),
        in_specs=ins,
        out_specs=tuple(spec for _, spec in outs),
        scratch_shapes=list(scratch),
        compiler_params=PARAMS,
        name=name,
    )


def per_device(tensor, factor_two, factor_three, factor_four):
    first, second, fourth, third = tensor.shape
    rank = factor_two.shape[1]
    wide = fourth * rank
    rows = first * second * fourth
    chunks = 8
    full = ((8, PACK + SUB, LANES), VMEM)
    short = ((8, PACK, LANES), VMEM)
    gram = ((SUB, LANES), VMEM)
    prod, sent, rest = call(
        functools.partial(root_kernel, first, chunks),
        "root",
        (((rows, wide), VMEM), full, gram),
        [HBM] * 4,
        (
            pltpu.VMEM((rows, third), jnp.bfloat16),
            pltpu.VMEM((rank, second), jnp.float32),
            pltpu.VMEM((rank, third), jnp.float32),
            pltpu.VMEM((fourth, rank), jnp.float32),
            pltpu.VMEM((first * SUB, wide), jnp.float32),
            pltpu.SemaphoreType.DMA((chunks + 3,)),
        ),
    )(*(held(x) for x in (tensor.reshape(rows, third), factor_two.T, factor_three.T, factor_four)))
    two = exchanged(sent, "ja")
    (sent,) = call(relay_kernel, "relay", (full,), [VMEM] * 2)(two, rest)
    got = exchanged(sent, "ka")
    new_one, sent, rest = call(
        functools.partial(middle_kernel, first, second, fourth),
        "middle",
        (((rank, first), HBM), full, gram),
        [VMEM] * 3,
        (
            pltpu.VMEM((rank, first), jnp.float32),
            pltpu.VMEM((first, wide), jnp.float32),
            pltpu.VMEM((second * fourth, wide), jnp.float32),
            pltpu.SemaphoreType.DMA,
        ),
    )(two, got, prod)
    one = exchanged(sent, "ia")
    (sent,) = call(relay_short_kernel, "relay_short", (short,), [VMEM])(one)
    got = exchanged(sent, "ka")
    (new_two,) = call(
        functools.partial(last_kernel, second), "last", (((rank, second), VMEM),), [VMEM] * 3
    )(one, rest, got)
    return (new_one.T, new_two.T)


def solution(mesh):
    return jax.shard_map(
        per_device,
        mesh=mesh,
        in_specs=(P("ia", "ja", None, "ka"), P("ja", None), P("ka", None), P()),
        out_specs=(P("ia", None), P("ja", None)),
        check_vma=False,
    )
```

time: 81.6 us -> 75.3 us (0.923)
  the two profiles are of different devices: /device:TPU:32 before, /device:TPU:1 now
where the time goes in v2:
time: 75.3 us; the launch traced here: 75 us
  blocking collectives  67.5 us (90%)
  Pallas kernels  6.88 us (9%)
    all_to_all x4, blocking collectives, exchanged(): return lax.all_to_all(array, axis, 0, 0, tiled=True)  67.5 us
    pallas_call x1, Pallas kernels, per_device(): call(functools.partial(root_kernel, first, chunks), 'root', (((rows, wide...  3.57 us
    pallas_call x1, Pallas kernels, per_device(): call(functools.partial(middle_kernel, first, second, fourth), 'middle', (...  1.76 us
    pallas_call x1, Pallas kernels, per_device(): call(functools.partial(last_kernel, second), 'last', (((rank, second), VM...  1.53 us

profile of v2, /device:TPU:1, one launch (start us, length us, event | category | flops | bytes accessed | tf_op | source)
XLA Modules:
  0.0 75.0 jit_solution(15503062242030825502)
XLA Ops:
  0.6 3.6 %root.1 = (f32[8192,64]{1,0:T(8,128)S(1)}, f32[8,24,128]{2,1,0:T(8,128)S(1)}, f32[8,128]{1,0:T(8,128)S(1)}) custom-call(bf16[8192,128]{1,0:T(8,128)(2,1)} %bitcast.5, f32[32,64]{1,0:T(8,128)} %bitcast.6, f32[32,128]{1,0:T(8,128)} %bitcast.7, f32[2,32]{1,0:T(2,128)} %f4_hbm.1), custom_call_target="tpu_custom_call" | custom-call | tf_op jit(solution)/shard_map/root/pallas_call | solution.py:235
  4.2 22.9 %all_to_all.20.in_ref.two_ref = f32[8,24,128]{2,1,0:T(8,128)S(1)} all-to-all(f32[8,24,128]{2,1,0:T(8,128)S(1)} %get-tuple-element.8), channel_id=1, replica_groups=mesh['ia'=8,'ja'=8,'ka'=8] {'ja'}, dimensions={0} | all-to-all | bytes 196608 | tf_op jit(solution)/shard_map/all_to_all | solution.py:211
  27.1 11.4 %all_to_all.21.in_ref = f32[8,24,128]{2,1,0:T(8,128)S(1)} all-to-all(f32[8,24,128]{2,1,0:T(8,128)S(1)} %relay.1), channel_id=1, replica_groups=mesh['ia'=8,'ja'=8,'ka'=8] {'ka'}, dimensions={0} | all-to-all | bytes 196608 | tf_op jit(solution)/shard_map/all_to_all | solution.py:211
  38.6 1.8 %middle.1 = (f32[32,64]{1,0:T(8,128)}, f32[8,24,128]{2,1,0:T(8,128)S(1)}, f32[8,128]{1,0:T(8,128)S(1)}) custom-call(f32[8,24,128]{2,1,0:T(8,128)S(1)} %all_to_all.20.in_ref.two_ref, f32[8,24,128]{2,1,0:T(8,128)S(1)} %all_to_all.21.in_ref, f32[8192,64]{1,0:T(8,128)S(1)} %get-tuple-element.10.prod_ref), custom_call_target="tpu_custom_call" | custom-call | tf_op jit(solution)/shard_map/middle/pallas_call | solution.py:252
  40.3 23.8 %all_to_all.22.in_ref.one_ref = f32[8,24,128]{2,1,0:T(8,128)S(1)} all-to-all(f32[8,24,128]{2,1,0:T(8,128)S(1)} %get-tuple-element.12), channel_id=1, replica_groups=mesh['ia'=8,'ja'=8,'ka'=8] {'ia'}, dimensions={0} | all-to-all | bytes 196608 | tf_op jit(solution)/shard_map/all_to_all | solution.py:211
  64.1 9.4 %all_to_all.23.in_ref = f32[8,16,128]{2,1,0:T(8,128)S(1)} all-to-all(f32[8,16,128]{2,1,0:T(8,128)S(1)} %relay_short.1), channel_id=1, replica_groups=mesh['ia'=8,'ja'=8,'ka'=8] {'ka'}, dimensions={0} | all-to-all | bytes 131072 | tf_op jit(solution)/shard_map/all_to_all | solution.py:211
  73.5 1.5 %last.1 = f32[32,64]{1,0:T(8,128)} custom-call(f32[8,24,128]{2,1,0:T(8,128)S(1)} %all_to_all.22.in_ref.one_ref, f32[8,128]{1,0:T(8,128)S(1)} %get-tuple-element.13.rest_ref, f32[8,16,128]{2,1,0:T(8,128)S(1)} %all_to_all.23.in_ref), custom_call_target="tpu_custom_call" | custom-call | tf_op jit(solution)/shard_map/last/pallas_call | solution.py:267
  (2 shorter events, 0.0 us)

commit v3 on v2

--- a/solution.py
+++ b/solution.py
@@ -11,6 +11,8 @@
 LANES = 128
 SUB = 8
 PACK = 16
+SLOTS = 8
+GROUPS = (3, 3, 2)
 VMEM = pl.BlockSpec(memory_space=pltpu.VMEM)
 HBM = pl.BlockSpec(memory_space=pltpu.HBM)
 PARAMS = pltpu.CompilerParams(vmem_limit_bytes=24 * 1024 * 1024)
@@ -32,17 +34,28 @@
 
 
 def fill_slots(out_ref, value, at=0):
-    for slot in range(out_ref.shape[0]):
-        out_ref[slot, at : at + value.shape[0], :] = value
+    step = out_ref.shape[0] // SLOTS
+    for slot in range(SLOTS):
+        out_ref[slot * step + at : slot * step + at + value.shape[0], :] = value
 
 
 def summed_slots(ref, lo, hi):
-    parts = [ref[s, lo:hi, :] for s in range(ref.shape[0])]
+    step = ref.shape[0] // SLOTS
+    parts = [ref[s * step + lo : s * step + hi, :] for s in range(SLOTS)]
     while len(parts) > 1:
         parts = [a + b for a, b in zip(parts[::2], parts[1::2])]
     return parts[0]
 
 
+def own_row(scratch_ref, value):
+    scratch_ref[...] = value
+    return scratch_ref[pl.ds(lax.axis_index("ka"), 1), :]
+
+
+def row_of_each(ref, at):
+    return ref[pl.ds(at, SLOTS, stride=ref.shape[0] // SLOTS), :]
+
+
 def packed(array, groups):
     rows = array.shape[0] // groups
     return jnp.concatenate([array[g * rows : (g + 1) * rows, :] for g in range(groups)], axis=1)
@@ -50,7 +63,7 @@
 
 def root_kernel(
     first, chunks, x_hbm, f2t_hbm, f3t_hbm, f4_hbm, prod_ref, pay_ref, rest_ref,
-    x_ref, f2t_ref, f3t_ref, f4_ref, r_ref, sems,
+    x_ref, f2t_ref, f3t_ref, f4_ref, r_ref, g_ref, sems,
 ):
     fourth, rank = f4_ref.shape
     second = f2t_ref.shape[1]
@@ -90,16 +103,19 @@
 
     gram_four = sum(cols[l] * f4[l : l + 1, :] for l in range(fourth))
     groups = rank // SUB
-    fill_slots(pay_ref, packed(contract_last(f2t, f2t), groups), PACK)
+    fill_slots(pay_ref, own_row(g_ref, packed(contract_last(f2t, f2t), groups)), PACK)
     rest_ref[...] = packed(contract_last(f3t, f3t) * gram_four, groups)
 
-    for c in range(chunks):
-        fetch(c).wait()
-        part = contract_last(x_ref[pl.ds(c * span, span), :], kt, None)
-        prod_ref[pl.ds(c * span, span), :] = part
-        r_ref[pl.ds(c * per * SUB, per * SUB), :] = jnp.sum(
-            part.reshape(per, rows // SUB, SUB, wide) * weight, axis=1
-        ).reshape(per * SUB, wide)
+    done = 0
+    for group in GROUPS:
+        for c in range(done, done + group):
+            fetch(c).wait()
+        part = contract_last(x_ref[pl.ds(done * span, group * span), :], kt, None)
+        prod_ref[pl.ds(done * span, group * span), :] = part
+        r_ref[pl.ds(done * per * SUB, group * per * SUB), :] = jnp.sum(
+            part.reshape(group * per, rows // SUB, SUB, wide) * weight, axis=1
+        ).reshape(group * per * SUB, wide)
+        done += group
 
     total = r_ref[pl.ds(0, first, stride=SUB), :]
     for s in range(1, SUB):
@@ -110,10 +126,12 @@
 def relay_kernel(in_ref, rest_ref, out_ref):
     fill_slots(out_ref, summed_slots(in_ref, 0, PACK))
     fill_slots(out_ref, rest_ref[...], PACK)
+    fill_slots(out_ref, summed_slots(in_ref, PACK, PACK + 1), PACK + SUB)
 
 
 def relay_short_kernel(in_ref, out_ref):
     fill_slots(out_ref, summed_slots(in_ref, 0, PACK))
+    fill_slots(out_ref, summed_slots(in_ref, PACK, PACK + 1), PACK)
 
 
 def eliminate(tiles, start, rank):
@@ -165,14 +183,14 @@
 
 
 def middle_kernel(
-    first, second, fourth, two_ref, in_ref, prod_ref, new_hbm, pay_ref, rest_ref,
-    new_ref, nx_ref, acc_ref, sem,
+    first, second, fourth, in_ref, prod_ref, new_hbm, pay_ref, rest_ref,
+    new_ref, nx_ref, acc_ref, g_ref, sem,
 ):
     rank = new_ref.shape[0]
     wide = fourth * rank
     rows = second * fourth
     rest = summed_slots(in_ref, PACK, PACK + SUB)
-    gram_two = summed_slots(two_ref, PACK, PACK + SUB)
+    gram_two = row_of_each(in_ref, PACK + SUB)
     rest_ref[...] = rest
     answer = solved(summed_slots(in_ref, 0, PACK), gram_two * rest, rank)[:, :first]
     new_ref[...] = answer
@@ -180,7 +198,7 @@
     leave.start()
     flat = jnp.transpose(answer)
     nx_ref[...] = jnp.concatenate([flat] * fourth, axis=1)
-    fill_slots(pay_ref, packed(contract_last(answer, answer), rank // SUB), PACK)
+    fill_slots(pay_ref, own_row(g_ref, packed(contract_last(answer, answer), rank // SUB)), PACK)
 
     def step(i, acc):
         at = pl.multiple_of(i * rows, rows)
@@ -197,18 +215,20 @@
     leave.wait()
 
 
-def last_kernel(second, one_ref, rest_ref, in_ref, new_ref):
-    gram_one = summed_slots(one_ref, PACK, PACK + SUB)
+def last_kernel(second, rest_ref, in_ref, new_ref):
+    gram_one = row_of_each(in_ref, PACK)
     rhs = summed_slots(in_ref, 0, PACK)
     new_ref[...] = solved(rhs, gram_one * rest_ref[...], new_ref.shape[0])[:, :second]
 
 
-def held(array):
-    return pltpu.with_memory_space_constraint(array, pltpu.HBM)
+def held(array, space=pltpu.HBM):
+    return pltpu.with_memory_space_constraint(array, space)
 
 
 def exchanged(array, axis):
-    return lax.all_to_all(array, axis, 0, 0, tiled=True)
+    rows, lanes = array.shape
+    slots = array.reshape(SLOTS, rows // SLOTS, 1, lanes)
+    return lax.all_to_all(slots, axis, 0, 0, tiled=True).reshape(rows, lanes)
 
 
 def call(kernel, name, outs, ins, scratch=()):
@@ -228,14 +248,14 @@
     rank = factor_two.shape[1]
     wide = fourth * rank
     rows = first * second * fourth
-    chunks = 8
-    full = ((8, PACK + SUB, LANES), VMEM)
-    short = ((8, PACK, LANES), VMEM)
+    chunks = sum(GROUPS)
+    narrow = ((SLOTS * (PACK + 1), LANES), VMEM)
+    full = ((SLOTS * (PACK + SUB + 1), LANES), VMEM)
     gram = ((SUB, LANES), VMEM)
     prod, sent, rest = call(
         functools.partial(root_kernel, first, chunks),
         "root",
-        (((rows, wide), VMEM), full, gram),
+        (((rows, wide), VMEM), narrow, gram),
         [HBM] * 4,
         (
             pltpu.VMEM((rows, third), jnp.bfloat16),
@@ -243,30 +263,32 @@
             pltpu.VMEM((rank, third), jnp.float32),
             pltpu.VMEM((fourth, rank), jnp.float32),
             pltpu.VMEM((first * SUB, wide), jnp.float32),
+            pltpu.VMEM((SUB, LANES), jnp.float32),
             pltpu.SemaphoreType.DMA((chunks + 3,)),
         ),
     )(*(held(x) for x in (tensor.reshape(rows, third), factor_two.T, factor_three.T, factor_four)))
-    two = exchanged(sent, "ja")
-    (sent,) = call(relay_kernel, "relay", (full,), [VMEM] * 2)(two, rest)
+    got = exchanged(sent, "ja")
+    (sent,) = call(relay_kernel, "relay", (full,), [VMEM] * 2)(got, rest)
     got = exchanged(sent, "ka")
     new_one, sent, rest = call(
         functools.partial(middle_kernel, first, second, fourth),
         "middle",
-        (((rank, first), HBM), full, gram),
-        [VMEM] * 3,
+        (((rank, first), HBM), narrow, gram),
+        [VMEM] * 2,
         (
             pltpu.VMEM((rank, first), jnp.float32),
             pltpu.VMEM((first, wide), jnp.float32),
             pltpu.VMEM((second * fourth, wide), jnp.float32),
+            pltpu.VMEM((SUB, LANES), jnp.float32),
             pltpu.SemaphoreType.DMA,
         ),
-    )(two, got, prod)
-    one = exchanged(sent, "ia")
-    (sent,) = call(relay_short_kernel, "relay_short", (short,), [VMEM])(one)
+    )(got, prod)
+    got = exchanged(sent, "ia")
+    (sent,) = call(relay_short_kernel, "relay_short", (narrow,), [VMEM])(got)
     got = exchanged(sent, "ka")
     (new_two,) = call(
-        functools.partial(last_kernel, second), "last", (((rank, second), VMEM),), [VMEM] * 3
-    )(one, rest, got)
+        functools.partial(last_kernel, second), "last", (((rank, second), VMEM),), [VMEM] * 2
+    )(rest, got)
     return (new_one.T, new_two.T)
 
 

time: 75.3 us -> 74.2 us (0.985)
  no operation moved by 1% of the time
where the time goes in v3:
time: 74.2 us; the launch traced here: 73.9 us
  blocking collectives  67 us (90%)
  Pallas kernels  6.3 us (8%)
    all_to_all x4, blocking collectives, exchanged(): return lax.all_to_all(slots, axis, 0, 0, tiled=True).reshape(rows, lanes)  67 us
    pallas_call x1, Pallas kernels, per_device(): call(functools.partial(root_kernel, first, chunks), 'root', (((rows, wide...  2.97 us
    pallas_call x1, Pallas kernels, per_device(): call(functools.partial(middle_kernel, first, second, fourth), 'middle', (...  1.78 us
    pallas_call x1, Pallas kernels, per_device(): call(functools.partial(last_kernel, second), 'last', (((rank, second), VM...  1.53 us

profile of v3, /device:TPU:1, one launch (start us, length us, event | category | flops | bytes accessed | tf_op | source)
XLA Modules:
  0.0 73.9 jit_solution(16927569906611559813)
XLA Ops:
  0.6 3.0 %root.1 = (f32[8192,64]{1,0:T(8,128)S(1)}, f32[136,128]{1,0:T(8,128)S(1)}, f32[8,128]{1,0:T(8,128)S(1)}) custom-call(bf16[8192,128]{1,0:T(8,128)(2,1)} %bitcast.21, f32[32,64]{1,0:T(8,128)} %bitcast.22, f32[32,128]{1,0:T(8,128)} %bitcast.23, f32[2,32]{1,0:T(2,128)} %f4_hbm.1), custom_call_target="tpu_custom_call" | custom-call | tf_op jit(solution)/shard_map/root/pallas_call | solution.py:255
  3.6 22.6 %all_to_all.20 = f32[8,17,1,128]{3,2,1,0:T(1,128)S(1)} all-to-all(f32[8,17,1,128]{3,2,1,0:T(1,128)S(1)} %bitcast.20), channel_id=1, replica_groups=mesh['ia'=8,'ja'=8,'ka'=8] {'ja'}, dimensions={0} | all-to-all | bytes 139264 | tf_op jit(solution)/shard_map/all_to_all | solution.py:231
  26.3 11.4 %all_to_all.21 = f32[8,25,1,128]{3,2,1,0:T(1,128)S(1)} all-to-all(f32[8,25,1,128]{3,2,1,0:T(1,128)S(1)} %bitcast.14), channel_id=1, replica_groups=mesh['ia'=8,'ja'=8,'ka'=8] {'ka'}, dimensions={0} | all-to-all | bytes 204800 | tf_op jit(solution)/shard_map/all_to_all | solution.py:231
  37.6 1.8 %middle.1 = (f32[32,64]{1,0:T(8,128)}, f32[136,128]{1,0:T(8,128)S(1)}, f32[8,128]{1,0:T(8,128)S(1)}) custom-call(f32[200,128]{1,0:T(8,128)S(1)} %bitcast.13, f32[8192,64]{1,0:T(8,128)S(1)} %get-tuple-element.10.prod_ref), custom_call_target="tpu_custom_call" | custom-call | tf_op jit(solution)/shard_map/middle/pallas_call | solution.py:273
  39.4 23.5 %all_to_all.22 = f32[8,17,1,128]{3,2,1,0:T(1,128)S(1)} all-to-all(f32[8,17,1,128]{3,2,1,0:T(1,128)S(1)} %bitcast.19), channel_id=1, replica_groups=mesh['ia'=8,'ja'=8,'ka'=8] {'ia'}, dimensions={0} | all-to-all | bytes 139264 | tf_op jit(solution)/shard_map/all_to_all | solution.py:231
  62.9 9.5 %all_to_all.23 = f32[8,17,1,128]{3,2,1,0:T(1,128)S(1)} all-to-all(f32[8,17,1,128]{3,2,1,0:T(1,128)S(1)} %bitcast.18), channel_id=1, replica_groups=mesh['ia'=8,'ja'=8,'ka'=8] {'ka'}, dimensions={0} | all-to-all | bytes 139264 | tf_op jit(solution)/shard_map/all_to_all | solution.py:231
  72.4 1.5 %last.1 = f32[32,64]{1,0:T(8,128)} custom-call(f32[8,128]{1,0:T(8,128)S(1)} %get-tuple-element.12.rest_ref, f32[136,128]{1,0:T(8,128)S(1)} %bitcast.16), custom_call_target="tpu_custom_call" | custom-call | tf_op jit(solution)/shard_map/last/pallas_call | solution.py:289
  (2 shorter events, 0.0 us)

commit v4 on v3

--- a/solution.py
+++ b/solution.py
@@ -12,7 +12,6 @@
 SUB = 8
 PACK = 16
 SLOTS = 8
-GROUPS = (3, 3, 2)
 VMEM = pl.BlockSpec(memory_space=pltpu.VMEM)
 HBM = pl.BlockSpec(memory_space=pltpu.HBM)
 PARAMS = pltpu.CompilerParams(vmem_limit_bytes=24 * 1024 * 1024)
@@ -28,9 +27,8 @@
     )
 
 
-def fold_matrix(rank, fourth):
-    shape = (rank, fourth * rank)
-    return (iota(shape, 1) % rank == iota(shape, 0)).astype(jnp.float32)
+def fold_matrix(rank, lanes):
+    return (iota((rank, lanes), 1) % rank == iota((rank, lanes), 0)).astype(jnp.float32)
 
 
 def fill_slots(out_ref, value, at=0):
@@ -66,11 +64,11 @@
     x_ref, f2t_ref, f3t_ref, f4_ref, r_ref, g_ref, sems,
 ):
     fourth, rank = f4_ref.shape
-    second = f2t_ref.shape[1]
+    second, third = f2t_ref.shape[1], f3t_ref.shape[1]
     wide = fourth * rank
     rows = second * fourth
-    per = first // chunks
-    span = per * rows
+    half = first // 2
+    span = first * rows // chunks
 
     def fetch(c):
         part = pl.ds(c * span, span)
@@ -95,32 +93,39 @@
         jnp.sum(jnp.where(eye, f4[l : l + 1, :], 0.0), axis=1, keepdims=True) for l in range(fourth)
     ]
     kt = jnp.concatenate([c * f3t for c in cols], axis=0).astype(jnp.bfloat16)
+    none = jnp.zeros_like(kt)
+    kt = jnp.concatenate(
+        [jnp.concatenate([kt, none], axis=1), jnp.concatenate([none, kt], axis=1)], axis=0
+    )
 
     spread = (iota((rows, second), 0) // fourth == iota((rows, second), 1)).astype(jnp.float32)
-    weight = contract_last(spread, jnp.concatenate([f2t] * fourth, axis=0))
-    keep = iota((rows, wide), 0) % fourth == iota((rows, wide), 1) // rank
-    weight = jnp.where(keep, weight, 0.0).reshape(1, rows // SUB, SUB, wide)
+    weight = contract_last(spread, jnp.concatenate([f2t] * (2 * fourth), axis=0))
+    keep = iota(weight.shape, 0) % fourth == iota(weight.shape, 1) // rank % fourth
+    weight = jnp.where(keep, weight, 0.0).reshape(1, rows // SUB, SUB, 2 * wide)
 
     gram_four = sum(cols[l] * f4[l : l + 1, :] for l in range(fourth))
     groups = rank // SUB
     fill_slots(pay_ref, own_row(g_ref, packed(contract_last(f2t, f2t), groups)), PACK)
     rest_ref[...] = packed(contract_last(f3t, f3t) * gram_four, groups)
 
-    done = 0
-    for group in GROUPS:
-        for c in range(done, done + group):
-            fetch(c).wait()
-        part = contract_last(x_ref[pl.ds(done * span, group * span), :], kt, None)
-        prod_ref[pl.ds(done * span, group * span), :] = part
-        r_ref[pl.ds(done * per * SUB, group * per * SUB), :] = jnp.sum(
-            part.reshape(group * per, rows // SUB, SUB, wide) * weight, axis=1
-        ).reshape(group * per * SUB, wide)
-        done += group
-
-    total = r_ref[pl.ds(0, first, stride=SUB), :]
+    for c in range(chunks):
+        fetch(c).wait()
+    pair = jnp.concatenate([x_ref[: half * rows, :], x_ref[half * rows :, :]], axis=1)
+    part = contract_last(pair, kt, None)
+    prod_ref[...] = part
+    r_ref[...] = jnp.sum(
+        part.reshape(half, rows // SUB, SUB, 2 * wide) * weight, axis=1
+    ).reshape(half * SUB, 2 * wide)
+
+    total = r_ref[pl.ds(0, half, stride=SUB), :]
     for s in range(1, SUB):
-        total = total + r_ref[pl.ds(s, first, stride=SUB), :]
-    fill_slots(pay_ref, packed(contract_last(fold_matrix(rank, fourth), total), 2))
+        total = total + r_ref[pl.ds(s, half, stride=SUB), :]
+    fold = fold_matrix(rank, 2 * wide)
+    side = iota(fold.shape, 1) // wide
+    folds = jnp.concatenate([jnp.where(side == h, fold, 0.0) for h in range(2)], axis=0)
+    sums = contract_last(folds, total)
+    quarters = [sums[h * rank + q : h * rank + q + PACK, :] for q in (0, PACK) for h in range(2)]
+    fill_slots(pay_ref, jnp.concatenate(quarters, axis=1))
 
 
 def relay_kernel(in_ref, rest_ref, out_ref):
@@ -197,7 +202,8 @@
     leave = pltpu.make_async_copy(new_ref, new_hbm, sem)
     leave.start()
     flat = jnp.transpose(answer)
-    nx_ref[...] = jnp.concatenate([flat] * fourth, axis=1)
+    half = first // 2
+    nx_ref[...] = jnp.concatenate([flat[:half]] * fourth + [flat[half:]] * fourth, axis=1)
     fill_slots(pay_ref, own_row(g_ref, packed(contract_last(answer, answer), rank // SUB)), PACK)
 
     def step(i, acc):
@@ -205,13 +211,13 @@
         return acc + prod_ref[pl.ds(at, rows), :] * nx_ref[pl.ds(i, 1), :]
 
     acc_ref[...] = lax.fori_loop(
-        0, first, step, jnp.zeros((rows, wide), jnp.float32), unroll=8
-    )
-    half = iota((second, wide), 1) // rank
+        0, half, step, jnp.zeros((rows, 2 * wide), jnp.float32), unroll=8
+    )
+    part = iota((second, 2 * wide), 1) // rank % fourth
     picked = acc_ref[pl.ds(0, second, stride=fourth), :]
     for l in range(1, fourth):
-        picked = jnp.where(half == l, acc_ref[pl.ds(l, second, stride=fourth), :], picked)
-    fill_slots(pay_ref, packed(contract_last(fold_matrix(rank, fourth), picked), 2))
+        picked = jnp.where(part == l, acc_ref[pl.ds(l, second, stride=fourth), :], picked)
+    fill_slots(pay_ref, packed(contract_last(fold_matrix(rank, 2 * wide), picked), 2))
     leave.wait()
 
 
@@ -246,23 +252,23 @@
 def per_device(tensor, factor_two, factor_three, factor_four):
     first, second, fourth, third = tensor.shape
     rank = factor_two.shape[1]
-    wide = fourth * rank
+    wide = 2 * fourth * rank
     rows = first * second * fourth
-    chunks = sum(GROUPS)
+    chunks = 8
     narrow = ((SLOTS * (PACK + 1), LANES), VMEM)
     full = ((SLOTS * (PACK + SUB + 1), LANES), VMEM)
     gram = ((SUB, LANES), VMEM)
     prod, sent, rest = call(
         functools.partial(root_kernel, first, chunks),
         "root",
-        (((rows, wide), VMEM), narrow, gram),
+        (((rows // 2, wide), VMEM), narrow, gram),
         [HBM] * 4,
         (
             pltpu.VMEM((rows, third), jnp.bfloat16),
             pltpu.VMEM((rank, second), jnp.float32),
             pltpu.VMEM((rank, third), jnp.float32),
             pltpu.VMEM((fourth, rank), jnp.float32),
-            pltpu.VMEM((first * SUB, wide), jnp.float32),
+            pltpu.VMEM((first // 2 * SUB, wide), jnp.float32),
             pltpu.VMEM((SUB, LANES), jnp.float32),
             pltpu.SemaphoreType.DMA((chunks + 3,)),
         ),
@@ -277,7 +283,7 @@
         [VMEM] * 2,
         (
             pltpu.VMEM((rank, first), jnp.float32),
-            pltpu.VMEM((first, wide), jnp.float32),
+            pltpu.VMEM((first // 2, wide), jnp.float32),
             pltpu.VMEM((second * fourth, wide), jnp.float32),
             pltpu.VMEM((SUB, LANES), jnp.float32),
             pltpu.SemaphoreType.DMA,

time: 74.2 us -> 73.8 us (level)
  no operation moved by 1% of the time
where the time goes in v4:
time: 73.8 us; the launch traced here: 73.5 us
  blocking collectives  67 us (91%)
  Pallas kernels  5.86 us (8%)
    all_to_all x4, blocking collectives, exchanged(): return lax.all_to_all(slots, axis, 0, 0, tiled=True).reshape(rows, lanes)  67 us
    pallas_call x1, Pallas kernels, per_device(): call(functools.partial(root_kernel, first, chunks), 'root', (((rows // 2,...  2.68 us
    pallas_call x1, Pallas kernels, per_device(): call(functools.partial(middle_kernel, first, second, fourth), 'middle', (...  1.63 us
    pallas_call x1, Pallas kernels, per_device(): call(functools.partial(last_kernel, second), 'last', (((rank, second), VM...  1.53 us

profile of v4, /device:TPU:1, one launch (start us, length us, event | category | flops | bytes accessed | tf_op | source)
XLA Modules:
  0.0 73.5 jit_solution(12292675641128327559)
XLA Ops:
  0.6 2.7 %root.1 = (f32[4096,128]{1,0:T(8,128)S(1)}, f32[136,128]{1,0:T(8,128)S(1)}, f32[8,128]{1,0:T(8,128)S(1)}) custom-call(bf16[8192,128]{1,0:T(8,128)(2,1)} %bitcast.21, f32[32,64]{1,0:T(8,128)} %bitcast.22, f32[32,128]{1,0:T(8,128)} %bitcast.23, f32[2,32]{1,0:T(2,128)} %f4_hbm.1), custom_call_target="tpu_custom_call" | custom-call | tf_op jit(solution)/shard_map/root/pallas_call | solution.py:261
  3.3 22.7 %all_to_all.20 = f32[8,17,1,128]{3,2,1,0:T(1,128)S(1)} all-to-all(f32[8,17,1,128]{3,2,1,0:T(1,128)S(1)} %bitcast.20), channel_id=1, replica_groups=mesh['ia'=8,'ja'=8,'ka'=8] {'ja'}, dimensions={0} | all-to-all | bytes 139264 | tf_op jit(solution)/shard_map/all_to_all | solution.py:237
  26.0 11.4 %all_to_all.21 = f32[8,25,1,128]{3,2,1,0:T(1,128)S(1)} all-to-all(f32[8,25,1,128]{3,2,1,0:T(1,128)S(1)} %bitcast.13), channel_id=1, replica_groups=mesh['ia'=8,'ja'=8,'ka'=8] {'ka'}, dimensions={0} | all-to-all | bytes 204800 | tf_op jit(solution)/shard_map/all_to_all | solution.py:237
  37.4 1.6 %middle.1 = (f32[32,64]{1,0:T(8,128)}, f32[136,128]{1,0:T(8,128)S(1)}, f32[8,128]{1,0:T(8,128)S(1)}) custom-call(f32[200,128]{1,0:T(8,128)S(1)} %bitcast.14, f32[4096,128]{1,0:T(8,128)S(1)} %get-tuple-element.10.prod_ref), custom_call_target="tpu_custom_call" | custom-call | tf_op jit(solution)/shard_map/middle/pallas_call | solution.py:279
  39.0 23.5 %all_to_all.22 = f32[8,17,1,128]{3,2,1,0:T(1,128)S(1)} all-to-all(f32[8,17,1,128]{3,2,1,0:T(1,128)S(1)} %bitcast.19), channel_id=1, replica_groups=mesh['ia'=8,'ja'=8,'ka'=8] {'ia'}, dimensions={0} | all-to-all | bytes 139264 | tf_op jit(solution)/shard_map/all_to_all | solution.py:237
  62.5 9.5 %all_to_all.23 = f32[8,17,1,128]{3,2,1,0:T(1,128)S(1)} all-to-all(f32[8,17,1,128]{3,2,1,0:T(1,128)S(1)} %bitcast.18), channel_id=1, replica_groups=mesh['ia'=8,'ja'=8,'ka'=8] {'ka'}, dimensions={0} | all-to-all | bytes 139264 | tf_op jit(solution)/shard_map/all_to_all | solution.py:237
  72.0 1.5 %last.1 = f32[32,64]{1,0:T(8,128)} custom-call(f32[8,128]{1,0:T(8,128)S(1)} %get-tuple-element.12.rest_ref, f32[136,128]{1,0:T(8,128)S(1)} %bitcast.16), custom_call_target="tpu_custom_call" | custom-call | tf_op jit(solution)/shard_map/last/pallas_call | solution.py:295
  (2 shorter events, 0.0 us)

commit v5 on v4

--- a/solution.py
+++ b/solution.py
@@ -5,6 +5,7 @@
 from jax import lax
 from jax.experimental import pallas as pl
 from jax.experimental.pallas import tpu as pltpu
+from jax.sharding import Mesh
 from jax.sharding import PartitionSpec as P
 
 HI = lax.Precision.HIGHEST
@@ -31,18 +32,21 @@
     return (iota((rank, lanes), 1) % rank == iota((rank, lanes), 0)).astype(jnp.float32)
 
 
-def fill_slots(out_ref, value, at=0):
-    step = out_ref.shape[0] // SLOTS
-    for slot in range(SLOTS):
+def fill_slots(out_ref, value, at=0, slots=SLOTS):
+    step = out_ref.shape[0] // slots
+    for slot in range(slots):
         out_ref[slot * step + at : slot * step + at + value.shape[0], :] = value
 
 
-def summed_slots(ref, lo, hi):
-    step = ref.shape[0] // SLOTS
-    parts = [ref[s * step + lo : s * step + hi, :] for s in range(SLOTS)]
+def total_of(parts):
     while len(parts) > 1:
-        parts = [a + b for a, b in zip(parts[::2], parts[1::2])]
+        parts = [sum(parts[n : n + 2]) for n in range(0, len(parts), 2)]
     return parts[0]
+
+
+def summed_slots(ref, lo, hi, slots=SLOTS):
+    step = ref.shape[0] // slots
+    return total_of([ref[s * step + lo : s * step + hi, :] for s in range(slots)])
 
 
 def own_row(scratch_ref, value):
@@ -50,8 +54,12 @@
     return scratch_ref[pl.ds(lax.axis_index("ka"), 1), :]
 
 
-def row_of_each(ref, at):
-    return ref[pl.ds(at, SLOTS, stride=ref.shape[0] // SLOTS), :]
+def row_of_each(ref, at, slots=SLOTS):
+    step = ref.shape[0] // slots
+    rows = [
+        ref[pl.ds(first * step + at, SLOTS, stride=step), :] for first in range(0, slots, SLOTS)
+    ]
+    return total_of(rows)
 
 
 def packed(array, groups):
@@ -134,9 +142,9 @@
     fill_slots(out_ref, summed_slots(in_ref, PACK, PACK + 1), PACK + SUB)
 
 
-def relay_short_kernel(in_ref, out_ref):
-    fill_slots(out_ref, summed_slots(in_ref, 0, PACK))
-    fill_slots(out_ref, summed_slots(in_ref, PACK, PACK + 1), PACK)
+def gather_kernel(slots, in_ref, out_ref):
+    out_ref[:PACK, :] = summed_slots(in_ref, 0, PACK, slots)
+    out_ref[PACK:, :] = row_of_each(in_ref, PACK, slots)
 
 
 def eliminate(tiles, start, rank):
@@ -188,7 +196,7 @@
 
 
 def middle_kernel(
-    first, second, fourth, in_ref, prod_ref, new_hbm, pay_ref, rest_ref,
+    first, second, fourth, slots, in_ref, prod_ref, new_hbm, pay_ref, rest_ref,
     new_ref, nx_ref, acc_ref, g_ref, sem,
 ):
     rank = new_ref.shape[0]
@@ -204,7 +212,8 @@
     flat = jnp.transpose(answer)
     half = first // 2
     nx_ref[...] = jnp.concatenate([flat[:half]] * fourth + [flat[half:]] * fourth, axis=1)
-    fill_slots(pay_ref, own_row(g_ref, packed(contract_last(answer, answer), rank // SUB)), PACK)
+    own = own_row(g_ref, packed(contract_last(answer, answer), rank // SUB))
+    fill_slots(pay_ref, own, PACK, slots)
 
     def step(i, acc):
         at = pl.multiple_of(i * rows, rows)
@@ -217,24 +226,25 @@
     picked = acc_ref[pl.ds(0, second, stride=fourth), :]
     for l in range(1, fourth):
         picked = jnp.where(part == l, acc_ref[pl.ds(l, second, stride=fourth), :], picked)
-    fill_slots(pay_ref, packed(contract_last(fold_matrix(rank, 2 * wide), picked), 2))
+    mode_two = contract_last(fold_matrix(rank, 2 * wide), picked)
+    fill_slots(pay_ref, packed(mode_two, 2), 0, slots)
     leave.wait()
 
 
-def last_kernel(second, rest_ref, in_ref, new_ref):
-    gram_one = row_of_each(in_ref, PACK)
-    rhs = summed_slots(in_ref, 0, PACK)
-    new_ref[...] = solved(rhs, gram_one * rest_ref[...], new_ref.shape[0])[:, :second]
+def last_kernel(second, rest_ref, own_ref, other_ref, new_ref):
+    value = own_ref[...] + other_ref[...]
+    gram = value[PACK:, :] * rest_ref[...]
+    new_ref[...] = solved(value[:PACK, :], gram, new_ref.shape[0])[:, :second]
 
 
 def held(array, space=pltpu.HBM):
     return pltpu.with_memory_space_constraint(array, space)
 
 
-def exchanged(array, axis):
+def exchanged(array, axes, slots=SLOTS):
     rows, lanes = array.shape
-    slots = array.reshape(SLOTS, rows // SLOTS, 1, lanes)
-    return lax.all_to_all(slots, axis, 0, 0, tiled=True).reshape(rows, lanes)
+    parts = array.reshape(slots, rows // slots, 1, lanes)
+    return lax.all_to_all(parts, axes, 0, 0, tiled=True).reshape(rows, lanes)
 
 
 def call(kernel, name, outs, ins, scratch=()):
@@ -276,10 +286,11 @@
     got = exchanged(sent, "ja")
     (sent,) = call(relay_kernel, "relay", (full,), [VMEM] * 2)(got, rest)
     got = exchanged(sent, "ka")
+    slots = lax.axis_size("x") * SLOTS
     new_one, sent, rest = call(
-        functools.partial(middle_kernel, first, second, fourth),
+        functools.partial(middle_kernel, first, second, fourth, slots),
         "middle",
-        (((rank, first), HBM), narrow, gram),
+        (((rank, first), HBM), ((slots * (PACK + 1), LANES), VMEM), gram),
         [VMEM] * 2,
         (
             pltpu.VMEM((rank, first), jnp.float32),
@@ -289,20 +300,24 @@
             pltpu.SemaphoreType.DMA,
         ),
     )(got, prod)
-    got = exchanged(sent, "ia")
-    (sent,) = call(relay_short_kernel, "relay_short", (narrow,), [VMEM])(got)
-    got = exchanged(sent, "ka")
+    got = exchanged(sent, ("x", "ka"), slots)
+    (own,) = call(
+        functools.partial(gather_kernel, slots), "gather", (((PACK + SUB, LANES), VMEM),), [VMEM]
+    )(got)
+    other = lax.ppermute(own, "zh", [(0, 1), (1, 0)])
     (new_two,) = call(
-        functools.partial(last_kernel, second), "last", (((rank, second), VMEM),), [VMEM] * 2
-    )(rest, got)
+        functools.partial(last_kernel, second), "last", (((rank, second), VMEM),), [VMEM] * 3
+    )(rest, own, other)
     return (new_one.T, new_two.T)
 
 
 def solution(mesh):
+    ia, ja, ka = (mesh.shape[name] for name in ("ia", "ja", "ka"))
+    parted = Mesh(mesh.devices.reshape(ia // 2, 2, ja, ka), ("x", "zh", "ja", "ka"))
     return jax.shard_map(
         per_device,
-        mesh=mesh,
-        in_specs=(P("ia", "ja", None, "ka"), P("ja", None), P("ka", None), P()),
-        out_specs=(P("ia", None), P("ja", None)),
+        mesh=parted,
+        in_specs=(P(("x", "zh"), "ja", None, "ka"), P("ja", None), P("ka", None), P()),
+        out_specs=(P(("x", "zh"), None), P("ja", None)),
         check_vma=False,
     )

time: 73.8 us -> 68.8 us (0.932)
  blocking collectives: 67 us -> 48.8 us
  starting transfers between devices: 0 us -> 7.94 us
  waiting for transfers between devices: 0 us -> 5.21 us
    all_to_all x4 -> x3, blocking collectives: 67 us -> 48.8 us  [exchanged(): return lax.all_to_all(parts, axes, 0, 0, tiled=True).reshape(rows, lanes)]
    ppermute x0 -> x1, starting transfers between devices: none -> 7.94 us  [per_device(): other = lax.ppermute(own, 'zh', [(0, 1), (1, 0)])]
    ppermute x0 -> x1, waiting for transfers between devices: none -> 5.21 us  [per_device(): other = lax.ppermute(own, 'zh', [(0, 1), (1, 0)])]
  transfers between devices with their start and end apart: 0 -> 1, of which waited for: 0 -> 1; matrix products, arithmetic and copies ran while one was open for 0% -> 0% of each run, Pallas kernels for 0% -> 0%
where the time goes in v5:
time: 68.8 us; the launch traced here: 68.5 us
  blocking collectives  48.8 us (71%)
  starting transfers between devices  7.94 us (12%)
  Pallas kernels  5.89 us (9%)
  waiting for transfers between devices  5.21 us (8%)
    all_to_all x3, blocking collectives, exchanged(): return lax.all_to_all(parts, axes, 0, 0, tiled=True).reshape(rows, lanes)  48.8 us
    ppermute x1, starting transfers between devices, per_device(): other = lax.ppermute(own, 'zh', [(0, 1), (1, 0)])  7.94 us
    ppermute x1, waiting for transfers between devices, per_device(): other = lax.ppermute(own, 'zh', [(0, 1), (1, 0)])  5.21 us
    pallas_call x1, Pallas kernels, per_device(): call(functools.partial(root_kernel, first, chunks), 'root', (((rows // 2,...  2.68 us
    pallas_call x1, Pallas kernels, per_device(): call(functools.partial(middle_kernel, first, second, fourth, slots), 'mid...  1.65 us
    pallas_call x1, Pallas kernels, per_device(): call(functools.partial(last_kernel, second), 'last', (((rank, second), VM...  1.53 us
  transfers between devices with their start and end apart: 1, of which 1 were waited for; matrix products, arithmetic and copies ran while one was open for 0% of the time, Pallas kernels for 0%

profile of v5, /device:TPU:1, one launch (start us, length us, event | category | flops | bytes accessed | tf_op | source)
XLA Modules:
  0.0 68.5 jit_solution(8382574692791445813)
XLA Ops:
  0.6 2.7 %root.1 = (f32[4096,128]{1,0:T(8,128)S(1)}, f32[136,128]{1,0:T(8,128)S(1)}, f32[8,128]{1,0:T(8,128)S(1)}) custom-call(bf16[8192,128]{1,0:T(8,128)(2,1)} %bitcast.17, f32[32,64]{1,0:T(8,128)} %bitcast.18, f32[32,128]{1,0:T(8,128)} %bitcast.19, f32[2,32]{1,0:T(2,128)} %f4_hbm.1), custom_call_target="tpu_custom_call" | custom-call | tf_op jit(solution)/shard_map/root/pallas_call | solution.py:271
  3.3 22.7 %all_to_all.15 = f32[8,17,1,128]{3,2,1,0:T(1,128)S(1)} all-to-all(f32[8,17,1,128]{3,2,1,0:T(1,128)S(1)} %bitcast.16), channel_id=1, replica_groups=mesh['x'=4,'zh'=2,'ja'=8,'ka'=8] {'ja'}, dimensions={0} | all-to-all | bytes 139264 | tf_op jit(solution)/shard_map/all_to_all | solution.py:247
  26.0 11.4 %all_to_all.16 = f32[8,25,1,128]{3,2,1,0:T(1,128)S(1)} all-to-all(f32[8,25,1,128]{3,2,1,0:T(1,128)S(1)} %bitcast.12), channel_id=1, replica_groups=mesh['x'=4,'zh'=2,'ja'=8,'ka'=8] {'ka'}, dimensions={0} | all-to-all | bytes 204800 | tf_op jit(solution)/shard_map/all_to_all | solution.py:247
  37.4 1.6 %middle.1 = (f32[32,64]{1,0:T(8,128)}, f32[544,128]{1,0:T(8,128)S(1)}, f32[8,128]{1,0:T(8,128)S(1)}) custom-call(f32[200,128]{1,0:T(8,128)S(1)} %bitcast.13, f32[4096,128]{1,0:T(8,128)S(1)} %get-tuple-element.10.prod_ref), custom_call_target="tpu_custom_call" | custom-call | tf_op jit(solution)/shard_map/middle/pallas_call | solution.py:290
  39.0 14.8 %all_to_all.17 = f32[32,17,1,128]{3,2,1,0:T(1,128)S(1)} all-to-all(f32[32,17,1,128]{3,2,1,0:T(1,128)S(1)} %bitcast.14), channel_id=1, replica_groups=mesh['x'=4,'zh'=2,'ja'=8,'ka'=8] {'x','ka'}, dimensions={0} | all-to-all | bytes 557056 | tf_op jit(solution)/shard_map/all_to_all | solution.py:247
  53.8 7.9 %collective-permute-start = (f32[24,128]{1,0:T(8,128)S(1)}, f32[24,128]{1,0:T(8,128)S(1)}, u32[]{:S(2)}, u32[]{:S(2)}) collective-permute-start(f32[24,128]{1,0:T(8,128)S(1)} %gather.1.own_ref), channel_id=1, source_target_pairs={{0,64},{64,0},{1,65},{65,1},{2,66},{66,2},{3,67},{67,3},{4,68},{68... | collective-permute-start | bytes 36872 | tf_op jit(solution)/shard_map/ppermute | solution.py:307
  61.8 5.2 %collective-permute-done.other_ref = f32[24,128]{1,0:T(8,128)S(1)} collective-permute-done((f32[24,128]{1,0:T(8,128)S(1)}, f32[24,128]{1,0:T(8,128)S(1)}, u32[]{:S(2)}, u32[]{:S(2)}) %collective-permute-start) | collective-permute-done | bytes 12320 | tf_op jit(solution)/shard_map/ppermute | solution.py:307
  67.0 1.5 %last.1 = f32[32,64]{1,0:T(8,128)} custom-call(f32[8,128]{1,0:T(8,128)S(1)} %get-tuple-element.12.rest_ref, f32[24,128]{1,0:T(8,128)S(1)} %gather.1.own_ref, f32[24,128]{1,0:T(8,128)S(1)} %collective-permute-done.other_ref), custom_call_target="tpu_custom_call" | custom-call | tf_op jit(solution)/shard_map/last/pallas_call | solution.py:308
  (2 shorter events, 0.0 us)
Async XLA Ops:
  53.8 13.2 %collective-permute-start = (f32[24,128]{1,0:T(8,128)S(1)}, f32[24,128]{1,0:T(8,128)S(1)}, u32[]{:S(2)}, u32[]{:S(2)}) collective-permute-start(f32[24,128]{1,0:T(8,128)S(1)} %gather.1.own_ref), channel_id=1, source_target_pairs={{0,64},{64,0},{1,65},{65,1},{2,66},{66,2},{3,67},{67,3},{4,68},{68... | collective-permute-start | bytes 36872 | tf_op jit(solution)/shard_map/ppermute | solution.py:307

commit v6 on v5

--- a/solution.py
+++ b/solution.py
@@ -49,9 +49,9 @@
     return total_of([ref[s * step + lo : s * step + hi, :] for s in range(slots)])
 
 
-def own_row(scratch_ref, value):
+def own_row(scratch_ref, value, lead):
     scratch_ref[...] = value
-    return scratch_ref[pl.ds(lax.axis_index("ka"), 1), :]
+    return scratch_ref[pl.ds((lax.axis_index("ka") + SLOTS - lead % SLOTS) % SLOTS, 1), :]
 
 
 def row_of_each(ref, at, slots=SLOTS):
@@ -113,7 +113,7 @@
 
     gram_four = sum(cols[l] * f4[l : l + 1, :] for l in range(fourth))
     groups = rank // SUB
-    fill_slots(pay_ref, own_row(g_ref, packed(contract_last(f2t, f2t), groups)), PACK)
+    fill_slots(pay_ref, own_row(g_ref, packed(contract_last(f2t, f2t), groups), KA_LEAD), PACK)
     rest_ref[...] = packed(contract_last(f3t, f3t) * gram_four, groups)
 
     for c in range(chunks):
@@ -212,7 +212,7 @@
     flat = jnp.transpose(answer)
     half = first // 2
     nx_ref[...] = jnp.concatenate([flat[:half]] * fourth + [flat[half:]] * fourth, axis=1)
-    own = own_row(g_ref, packed(contract_last(answer, answer), rank // SUB))
+    own = own_row(g_ref, packed(contract_last(answer, answer), rank // SUB), X_LEAD)
     fill_slots(pay_ref, own, PACK, slots)
 
     def step(i, acc):
@@ -241,10 +241,21 @@
     return pltpu.with_memory_space_constraint(array, space)
 
 
-def exchanged(array, axes, slots=SLOTS):
+JA_ORDER = ((7, 6, 5, 4, 3, 2, 1, 0), (7, 6, 5, 4, 3, 2, 1, 0))
+KA_LEAD = 5
+X_LEAD = 21
+
+
+def rotated(count, lead):
+    return [[(n + lead) % count for n in range(count)]]
+
+
+def exchanged(array, axes, groups):
+    slots = len(groups[0])
     rows, lanes = array.shape
     parts = array.reshape(slots, rows // slots, 1, lanes)
-    return lax.all_to_all(parts, axes, 0, 0, tiled=True).reshape(rows, lanes)
+    swapped = lax.all_to_all(parts, axes, 0, 0, tiled=True, axis_index_groups=groups)
+    return swapped.reshape(rows, lanes)
 
 
 def call(kernel, name, outs, ins, scratch=()):
@@ -283,9 +294,9 @@
             pltpu.SemaphoreType.DMA((chunks + 3,)),
         ),
     )(*(held(x) for x in (tensor.reshape(rows, third), factor_two.T, factor_three.T, factor_four)))
-    got = exchanged(sent, "ja")
+    got = exchanged(sent, ("zh", "ja"), [[h * SLOTS + j for j in JA_ORDER[h]] for h in range(2)])
     (sent,) = call(relay_kernel, "relay", (full,), [VMEM] * 2)(got, rest)
-    got = exchanged(sent, "ka")
+    got = exchanged(sent, "ka", rotated(SLOTS, KA_LEAD))
     slots = lax.axis_size("x") * SLOTS
     new_one, sent, rest = call(
         functools.partial(middle_kernel, first, second, fourth, slots),
@@ -300,7 +311,7 @@
             pltpu.SemaphoreType.DMA,
         ),
     )(got, prod)
-    got = exchanged(sent, ("x", "ka"), slots)
+    got = exchanged(sent, ("x", "ka"), rotated(slots, X_LEAD))
     (own,) = call(
         functools.partial(gather_kernel, slots), "gather", (((PACK + SUB, LANES), VMEM),), [VMEM]
     )(got)

time: 68.8 us -> 59.3 us (0.86)
  blocking collectives: 48.8 us -> 39 us
  starting transfers between devices: 7.94 us -> 11.2 us
  waiting for transfers between devices: 5.21 us -> 1.99 us
    all_to_all x3, blocking collectives: 48.8 us -> 39 us  [exchanged(): lax.all_to_all(parts, axes, 0, 0, tiled=True, axis_index_groups=groups)]
    ppermute x1, starting transfers between devices: 7.94 us -> 11.2 us  [per_device(): other = lax.ppermute(own, 'zh', [(0, 1), (1, 0)])]
    ppermute x1, waiting for transfers between devices: 5.21 us -> 1.99 us  [per_device(): other = lax.ppermute(own, 'zh', [(0, 1), (1, 0)])]
where the time goes in v6:
time: 59.3 us; the launch traced here: 58.7 us
  blocking collectives  39 us (66%)
  starting transfers between devices  11.2 us (19%)
  Pallas kernels  5.89 us (10%)
  waiting for transfers between devices  1.99 us (3%)
  between operations  0.66 us (1%)
    all_to_all x3, blocking collectives, exchanged(): lax.all_to_all(parts, axes, 0, 0, tiled=True, axis_index_groups=groups)  39 us
    ppermute x1, starting transfers between devices, per_device(): other = lax.ppermute(own, 'zh', [(0, 1), (1, 0)])  11.2 us
    pallas_call x1, Pallas kernels, per_device(): call(functools.partial(root_kernel, first, chunks), 'root', (((rows // 2,...  2.68 us
    ppermute x1, waiting for transfers between devices, per_device(): other = lax.ppermute(own, 'zh', [(0, 1), (1, 0)])  1.99 us
    pallas_call x1, Pallas kernels, per_device(): call(functools.partial(middle_kernel, first, second, fourth, slots), 'mid...  1.65 us
    pallas_call x1, Pallas kernels, per_device(): call(functools.partial(last_kernel, second), 'last', (((rank, second), VM...  1.53 us
  transfers between devices with their start and end apart: 1, of which 1 were waited for; matrix products, arithmetic and copies ran while one was open for 0% of the time, Pallas kernels for 0%

profile of v6, /device:TPU:1, one launch (start us, length us, event | category | flops | bytes accessed | tf_op | source)
XLA Modules:
  0.0 58.7 jit_solution(1359859373321968592)
XLA Ops:
  0.6 2.7 %root.1 = (f32[4096,128]{1,0:T(8,128)S(1)}, f32[136,128]{1,0:T(8,128)S(1)}, f32[8,128]{1,0:T(8,128)S(1)}) custom-call(bf16[8192,128]{1,0:T(8,128)(2,1)} %bitcast.17, f32[32,64]{1,0:T(8,128)} %bitcast.18, f32[32,128]{1,0:T(8,128)} %bitcast.19, f32[2,32]{1,0:T(2,128)} %f4_hbm.1), custom_call_target="tpu_custom_call" | custom-call | tf_op jit(solution)/shard_map/root/pallas_call | solution.py:282
  3.3 17.2 %all_to_all.15 = f32[8,17,1,128]{3,2,1,0:T(1,128)S(1)} all-to-all(f32[8,17,1,128]{3,2,1,0:T(1,128)S(1)} %bitcast.16), channel_id=1, replica_groups={{56,48,40,32,24,16,8,0},{120,112,104,96,88,80,72,64},{57,49,41,33,25,17..., dimensions={0} | all-to-all | bytes 139264 | tf_op jit(solution)/shard_map/all_to_all | solution.py:257
  20.6 9.5 %all_to_all.16 = f32[8,25,1,128]{3,2,1,0:T(1,128)S(1)} all-to-all(f32[8,25,1,128]{3,2,1,0:T(1,128)S(1)} %bitcast.12), channel_id=1, replica_groups={{5,6,7,0,1,2,3,4},{13,14,15,8,9,10,11,12},{21,22,23,16,17,18,19,20},{29..., dimensions={0} | all-to-all | bytes 204800 | tf_op jit(solution)/shard_map/all_to_all | solution.py:257
  30.0 1.6 %middle.1 = (f32[32,64]{1,0:T(8,128)}, f32[544,128]{1,0:T(8,128)S(1)}, f32[8,128]{1,0:T(8,128)S(1)}) custom-call(f32[200,128]{1,0:T(8,128)S(1)} %bitcast.13, f32[4096,128]{1,0:T(8,128)S(1)} %get-tuple-element.10.prod_ref), custom_call_target="tpu_custom_call" | custom-call | tf_op jit(solution)/shard_map/middle/pallas_call | solution.py:301
  31.7 12.3 %all_to_all.17 = f32[32,17,1,128]{3,2,1,0:T(1,128)S(1)} all-to-all(f32[32,17,1,128]{3,2,1,0:T(1,128)S(1)} %bitcast.14), channel_id=1, replica_groups={{261,262,263,384,385,386,387,388,389,390,391,0,1,2,3,4,5,6,7,128,129,13..., dimensions={0} | all-to-all | bytes 557056 | tf_op jit(solution)/shard_map/all_to_all | solution.py:257
  44.0 11.2 %collective-permute-start = (f32[24,128]{1,0:T(8,128)S(1)}, f32[24,128]{1,0:T(8,128)S(1)}, u32[]{:S(2)}, u32[]{:S(2)}) collective-permute-start(f32[24,128]{1,0:T(8,128)S(1)} %gather.1.own_ref), channel_id=1, source_target_pairs={{0,64},{64,0},{1,65},{65,1},{2,66},{66,2},{3,67},{67,3},{4,68},{68... | collective-permute-start | bytes 36872 | tf_op jit(solution)/shard_map/ppermute | solution.py:318
  55.2 2.0 %collective-permute-done.other_ref = f32[24,128]{1,0:T(8,128)S(1)} collective-permute-done((f32[24,128]{1,0:T(8,128)S(1)}, f32[24,128]{1,0:T(8,128)S(1)}, u32[]{:S(2)}, u32[]{:S(2)}) %collective-permute-start) | collective-permute-done | bytes 12320 | tf_op jit(solution)/shard_map/ppermute | solution.py:318
  57.2 1.5 %last.1 = f32[32,64]{1,0:T(8,128)} custom-call(f32[8,128]{1,0:T(8,128)S(1)} %get-tuple-element.12.rest_ref, f32[24,128]{1,0:T(8,128)S(1)} %gather.1.own_ref, f32[24,128]{1,0:T(8,128)S(1)} %collective-permute-done.other_ref), custom_call_target="tpu_custom_call" | custom-call | tf_op jit(solution)/shard_map/last/pallas_call | solution.py:319
  (2 shorter events, 0.0 us)
Async XLA Ops:
  44.0 13.2 %collective-permute-start = (f32[24,128]{1,0:T(8,128)S(1)}, f32[24,128]{1,0:T(8,128)S(1)}, u32[]{:S(2)}, u32[]{:S(2)}) collective-permute-start(f32[24,128]{1,0:T(8,128)S(1)} %gather.1.own_ref), channel_id=1, source_target_pairs={{0,64},{64,0},{1,65},{65,1},{2,66},{66,2},{3,67},{67,3},{4,68},{68... | collective-permute-start | bytes 36872 | tf_op jit(solution)/shard_map/ppermute | solution.py:318

commit v7 on v4

--- a/solution.py
+++ b/solution.py
@@ -5,6 +5,7 @@
 from jax import lax
 from jax.experimental import pallas as pl
 from jax.experimental.pallas import tpu as pltpu
+from jax.sharding import Mesh
 from jax.sharding import PartitionSpec as P
 
 HI = lax.Precision.HIGHEST
@@ -45,9 +46,9 @@
     return parts[0]
 
 
-def own_row(scratch_ref, value):
+def own_row(scratch_ref, value, lead):
     scratch_ref[...] = value
-    return scratch_ref[pl.ds(lax.axis_index("ka"), 1), :]
+    return scratch_ref[pl.ds((lax.axis_index("ka") + SLOTS - lead) % SLOTS, 1), :]
 
 
 def row_of_each(ref, at):
@@ -105,7 +106,7 @@
 
     gram_four = sum(cols[l] * f4[l : l + 1, :] for l in range(fourth))
     groups = rank // SUB
-    fill_slots(pay_ref, own_row(g_ref, packed(contract_last(f2t, f2t), groups)), PACK)
+    fill_slots(pay_ref, own_row(g_ref, packed(contract_last(f2t, f2t), groups), KA_FIRST[0]), PACK)
     rest_ref[...] = packed(contract_last(f3t, f3t) * gram_four, groups)
 
     for c in range(chunks):
@@ -204,7 +205,7 @@
     flat = jnp.transpose(answer)
     half = first // 2
     nx_ref[...] = jnp.concatenate([flat[:half]] * fourth + [flat[half:]] * fourth, axis=1)
-    fill_slots(pay_ref, own_row(g_ref, packed(contract_last(answer, answer), rank // SUB)), PACK)
+    fill_slots(pay_ref, own_row(g_ref, packed(contract_last(answer, answer), rank // SUB), KA_FIRST[1]), PACK)
 
     def step(i, acc):
         at = pl.multiple_of(i * rows, rows)
@@ -231,10 +232,20 @@
     return pltpu.with_memory_space_constraint(array, space)
 
 
-def exchanged(array, axis):
+JA_ORDER = ((7, 6, 5, 4, 3, 2, 1, 0), (5, 4, 6, 3, 7, 2, 1, 0))
+IA_ORDER = (5, 7, 3, 1, 4, 6, 2, 0)
+KA_FIRST = (5, 5)
+
+
+def rotated(lead):
+    return [[(n + lead) % SLOTS for n in range(SLOTS)]]
+
+
+def exchanged(array, axes, groups):
     rows, lanes = array.shape
-    slots = array.reshape(SLOTS, rows // SLOTS, 1, lanes)
-    return lax.all_to_all(slots, axis, 0, 0, tiled=True).reshape(rows, lanes)
+    parts = array.reshape(SLOTS, rows // SLOTS, 1, lanes)
+    swapped = lax.all_to_all(parts, axes, 0, 0, tiled=True, axis_index_groups=groups)
+    return swapped.reshape(rows, lanes)
 
 
 def call(kernel, name, outs, ins, scratch=()):
@@ -273,9 +284,9 @@
             pltpu.SemaphoreType.DMA((chunks + 3,)),
         ),
     )(*(held(x) for x in (tensor.reshape(rows, third), factor_two.T, factor_three.T, factor_four)))
-    got = exchanged(sent, "ja")
+    got = exchanged(sent, ("zh", "ja"), [[h * SLOTS + j for j in JA_ORDER[h]] for h in range(2)])
     (sent,) = call(relay_kernel, "relay", (full,), [VMEM] * 2)(got, rest)
-    got = exchanged(sent, "ka")
+    got = exchanged(sent, "ka", rotated(KA_FIRST[0]))
     new_one, sent, rest = call(
         functools.partial(middle_kernel, first, second, fourth),
         "middle",
@@ -289,9 +300,9 @@
             pltpu.SemaphoreType.DMA,
         ),
     )(got, prod)
-    got = exchanged(sent, "ia")
+    got = exchanged(sent, ("x", "zh"), [IA_ORDER])
     (sent,) = call(relay_short_kernel, "relay_short", (narrow,), [VMEM])(got)
-    got = exchanged(sent, "ka")
+    got = exchanged(sent, "ka", rotated(KA_FIRST[1]))
     (new_two,) = call(
         functools.partial(last_kernel, second), "last", (((rank, second), VMEM),), [VMEM] * 2
     )(rest, got)
@@ -299,10 +310,12 @@
 
 
 def solution(mesh):
+    ia, ja, ka = (mesh.shape[name] for name in ("ia", "ja", "ka"))
+    parted = Mesh(mesh.devices.reshape(ia // 2, 2, ja, ka), ("x", "zh", "ja", "ka"))
     return jax.shard_map(
         per_device,
-        mesh=mesh,
-        in_specs=(P("ia", "ja", None, "ka"), P("ja", None), P("ka", None), P()),
-        out_specs=(P("ia", None), P("ja", None)),
+        mesh=parted,
+        in_specs=(P(("x", "zh"), "ja", None, "ka"), P("ja", None), P("ka", None), P()),
+        out_specs=(P(("x", "zh"), None), P("ja", None)),
         check_vma=False,
     )

time: 73.8 us -> 58.3 us (0.79)
  blocking collectives: 67 us -> 51.5 us
    all_to_all x4, blocking collectives: 67 us -> 51.5 us  [exchanged(): lax.all_to_all(parts, axes, 0, 0, tiled=True, axis_index_groups=groups)]
where the time goes in v7:
time: 58.3 us; the launch traced here: 58 us
  blocking collectives  51.5 us (88%)
  Pallas kernels  5.86 us (10%)
  between operations  0.66 us (1%)
    all_to_all x4, blocking collectives, exchanged(): lax.all_to_all(parts, axes, 0, 0, tiled=True, axis_index_groups=groups)  51.5 us
    pallas_call x1, Pallas kernels, per_device(): call(functools.partial(root_kernel, first, chunks), 'root', (((rows // 2,...  2.68 us
    pallas_call x1, Pallas kernels, per_device(): call(functools.partial(middle_kernel, first, second, fourth), 'middle', (...  1.63 us
    pallas_call x1, Pallas kernels, per_device(): call(functools.partial(last_kernel, second), 'last', (((rank, second), VM...  1.53 us

profile of v7, /device:TPU:1, one launch (start us, length us, event | category | flops | bytes accessed | tf_op | source)
XLA Modules:
  0.0 58.0 jit_solution(10506434076747006037)
XLA Ops:
  0.6 2.7 %root.1 = (f32[4096,128]{1,0:T(8,128)S(1)}, f32[136,128]{1,0:T(8,128)S(1)}, f32[8,128]{1,0:T(8,128)S(1)}) custom-call(bf16[8192,128]{1,0:T(8,128)(2,1)} %bitcast.21, f32[32,64]{1,0:T(8,128)} %bitcast.22, f32[32,128]{1,0:T(8,128)} %bitcast.23, f32[2,32]{1,0:T(2,128)} %f4_hbm.1), custom_call_target="tpu_custom_call" | custom-call | tf_op jit(solution)/shard_map/root/pallas_call | solution.py:272
  3.3 17.2 %all_to_all.20 = f32[8,17,1,128]{3,2,1,0:T(1,128)S(1)} all-to-all(f32[8,17,1,128]{3,2,1,0:T(1,128)S(1)} %bitcast.20), channel_id=1, replica_groups={{56,48,40,32,24,16,8,0},{104,96,112,88,120,80,72,64},{57,49,41,33,25,17..., dimensions={0} | all-to-all | bytes 139264 | tf_op jit(solution)/shard_map/all_to_all | solution.py:247
  20.6 9.5 %all_to_all.21 = f32[8,25,1,128]{3,2,1,0:T(1,128)S(1)} all-to-all(f32[8,25,1,128]{3,2,1,0:T(1,128)S(1)} %bitcast.13), channel_id=1, replica_groups={{5,6,7,0,1,2,3,4},{13,14,15,8,9,10,11,12},{21,22,23,16,17,18,19,20},{29..., dimensions={0} | all-to-all | bytes 204800 | tf_op jit(solution)/shard_map/all_to_all | solution.py:247
  30.0 1.6 %middle.1 = (f32[32,64]{1,0:T(8,128)}, f32[136,128]{1,0:T(8,128)S(1)}, f32[8,128]{1,0:T(8,128)S(1)}) custom-call(f32[200,128]{1,0:T(8,128)S(1)} %bitcast.14, f32[4096,128]{1,0:T(8,128)S(1)} %get-tuple-element.10.prod_ref), custom_call_target="tpu_custom_call" | custom-call | tf_op jit(solution)/shard_map/middle/pallas_call | solution.py:290
  31.7 16.4 %all_to_all.22 = f32[8,17,1,128]{3,2,1,0:T(1,128)S(1)} all-to-all(f32[8,17,1,128]{3,2,1,0:T(1,128)S(1)} %bitcast.19), channel_id=1, replica_groups={{320,448,192,64,256,384,128,0},{321,449,193,65,257,385,129,1},{322,450,..., dimensions={0} | all-to-all | bytes 139264 | tf_op jit(solution)/shard_map/all_to_all | solution.py:247
  48.1 8.4 %all_to_all.23 = f32[8,17,1,128]{3,2,1,0:T(1,128)S(1)} all-to-all(f32[8,17,1,128]{3,2,1,0:T(1,128)S(1)} %bitcast.18), channel_id=1, replica_groups={{5,6,7,0,1,2,3,4},{13,14,15,8,9,10,11,12},{21,22,23,16,17,18,19,20},{29..., dimensions={0} | all-to-all | bytes 139264 | tf_op jit(solution)/shard_map/all_to_all | solution.py:247
  56.5 1.5 %last.1 = f32[32,64]{1,0:T(8,128)} custom-call(f32[8,128]{1,0:T(8,128)S(1)} %get-tuple-element.12.rest_ref, f32[136,128]{1,0:T(8,128)S(1)} %bitcast.16), custom_call_target="tpu_custom_call" | custom-call | tf_op jit(solution)/shard_map/last/pallas_call | solution.py:306
  (2 shorter events, 0.0 us)

commit v8 on v7

--- a/solution.py
+++ b/solution.py
@@ -12,6 +12,7 @@
 LANES = 128
 SUB = 8
 PACK = 16
+PAIR = 2
 SLOTS = 8
 VMEM = pl.BlockSpec(memory_space=pltpu.VMEM)
 HBM = pl.BlockSpec(memory_space=pltpu.HBM)
@@ -28,8 +29,32 @@
     )
 
 
-def fold_matrix(rank, lanes):
-    return (iota((rank, lanes), 1) % rank == iota((rank, lanes), 0)).astype(jnp.float32)
+def pieces(array):
+    out = []
+    for _ in range(3):
+        part = array.astype(jnp.bfloat16)
+        out.append(part)
+        array = array - part.astype(jnp.float32)
+    return out
+
+
+def packed_sums(rows, rank, keeps):
+    lanes = rows.shape[1]
+    halves = rank // PACK
+    where = (PACK, halves * lanes)
+    half, lane = iota(where, 1) // lanes, iota(where, 1) % lanes
+    picks = (lane % rank == iota(where, 0) + PACK * half).astype(jnp.bfloat16)
+    total = None
+    for part in pieces(rows):
+        blocks = []
+        none = jnp.zeros_like(part)
+        for h in range(halves):
+            for keep in keeps:
+                kept = part if keep is None else jnp.where(keep, part, none)
+                blocks.append(jnp.concatenate([kept if g == h else none for g in range(halves)], axis=1))
+        term = contract_last(picks, jnp.concatenate(blocks, axis=0), None)
+        total = term if total is None else total + term
+    return total
 
 
 def fill_slots(out_ref, value, at=0):
@@ -121,12 +146,8 @@
     total = r_ref[pl.ds(0, half, stride=SUB), :]
     for s in range(1, SUB):
         total = total + r_ref[pl.ds(s, half, stride=SUB), :]
-    fold = fold_matrix(rank, 2 * wide)
-    side = iota(fold.shape, 1) // wide
-    folds = jnp.concatenate([jnp.where(side == h, fold, 0.0) for h in range(2)], axis=0)
-    sums = contract_last(folds, total)
-    quarters = [sums[h * rank + q : h * rank + q + PACK, :] for q in (0, PACK) for h in range(2)]
-    fill_slots(pay_ref, jnp.concatenate(quarters, axis=1))
+    side = iota(total.shape, 1) // wide
+    fill_slots(pay_ref, packed_sums(total, rank, [side == h for h in range(2)]))
 
 
 def relay_kernel(in_ref, rest_ref, out_ref):
@@ -144,32 +165,42 @@
     lanes = tiles[0].shape[1]
     count = rank // SUB
     row = iota((SUB, lanes), 0)
-    for b in range(count):
+    width = PAIR * SUB
+    for b in range(0, count, PAIR):
+        first = start + b * SUB
         cols = [
             [
-                jnp.broadcast_to(tiles[t][:, start + b * SUB + c : start + b * SUB + c + 1], (SUB, lanes))
-                for c in range(SUB)
+                jnp.broadcast_to(tile[:, first + c : first + c + 1], (SUB, lanes))
+                for c in range(width)
             ]
-            for t in range(count)
+            for tile in tiles
         ]
-        own = tiles[b]
-        piv = cols[b]
-        for c in range(SUB):
-            factor = piv[c]
-            inverse = 1.0 / factor[c : c + 1, :]
-            lead = own[c : c + 1, :] * inverse
-            here = row == c
-            own = jnp.where(here, lead, own - factor * lead)
-            for d in range(c + 1, SUB):
-                lead_d = piv[d][c : c + 1, :] * inverse
-                piv[d] = jnp.where(here, lead_d, piv[d] - factor * lead_d)
-        tiles[b] = own
+        own = tiles[b : b + PAIR]
+        piv = [list(cols[b + k]) for k in range(PAIR)]
+        for c in range(width):
+            home, r = c // SUB, c % SUB
+            here = row == r
+            factors = [piv[k][c] for k in range(PAIR)]
+            inverse = 1.0 / factors[home][r : r + 1, :]
+
+            def cleared(column):
+                lead = column[home][r : r + 1, :] * inverse
+                rest = [column[k] - factors[k] * lead for k in range(PAIR)]
+                rest[home] = jnp.where(here, lead, rest[home])
+                return rest
+
+            own = cleared(own)
+            for d in range(c + 1, width):
+                for k, value in enumerate(cleared([piv[k][d] for k in range(PAIR)])):
+                    piv[k][d] = value
         for t in range(count):
-            if t != b:
-                acc = tiles[t]
-                for c in range(SUB):
-                    acc = acc - cols[t][c] * own[c : c + 1, :]
-                tiles[t] = acc
+            if b <= t < b + PAIR:
+                tiles[t] = own[t - b]
+            else:
+                terms = [cols[t][c] * own[c // SUB][c % SUB : c % SUB + 1, :] for c in range(width)]
+                while len(terms) > 1:
+                    terms = [x + y for x, y in zip(terms[::2], terms[1::2])]
+                tiles[t] = tiles[t] - terms[0]
     return tiles
 
 
@@ -218,7 +249,7 @@
     picked = acc_ref[pl.ds(0, second, stride=fourth), :]
     for l in range(1, fourth):
         picked = jnp.where(part == l, acc_ref[pl.ds(l, second, stride=fourth), :], picked)
-    fill_slots(pay_ref, packed(contract_last(fold_matrix(rank, 2 * wide), picked), 2))
+    fill_slots(pay_ref, packed_sums(picked, rank, [None]))
     leave.wait()
 
 
@@ -233,7 +264,7 @@
 
 
 JA_ORDER = ((7, 6, 5, 4, 3, 2, 1, 0), (5, 4, 6, 3, 7, 2, 1, 0))
-IA_ORDER = (5, 7, 3, 1, 4, 6, 2, 0)
+IA_ORDER = (5, 4, 6, 2, 0, 7, 3, 1)
 KA_FIRST = (5, 5)
 
 

time: 58.3 us -> 57.6 us (0.988)
  Pallas kernels: 5.86 us -> 5.25 us
where the time goes in v8:
time: 57.6 us; the launch traced here: 57.3 us
  blocking collectives  51.4 us (89%)
  Pallas kernels  5.25 us (9%)
  between operations  0.66 us (1%)
    all_to_all x4, blocking collectives, exchanged(): lax.all_to_all(parts, axes, 0, 0, tiled=True, axis_index_groups=groups)  51.4 us
    pallas_call x1, Pallas kernels, per_device(): call(functools.partial(root_kernel, first, chunks), 'root', (((rows // 2,...  2.67 us
    pallas_call x1, Pallas kernels, per_device(): call(functools.partial(middle_kernel, first, second, fourth), 'middle', (...  1.28 us
    pallas_call x1, Pallas kernels, per_device(): call(functools.partial(last_kernel, second), 'last', (((rank, second), VM...  1.27 us

profile of v8, /device:TPU:1, one launch (start us, length us, event | category | flops | bytes accessed | tf_op | source)
XLA Modules:
  0.0 57.3 jit_solution(17978548473253084781)
XLA Ops:
  0.6 2.7 %root.1 = (f32[4096,128]{1,0:T(8,128)S(1)}, f32[136,128]{1,0:T(8,128)S(1)}, f32[8,128]{1,0:T(8,128)S(1)}) custom-call(bf16[8192,128]{1,0:T(8,128)(2,1)} %bitcast.21, f32[32,64]{1,0:T(8,128)} %bitcast.22, f32[32,128]{1,0:T(8,128)} %bitcast.23, f32[2,32]{1,0:T(2,128)} %f4_hbm.1), custom_call_target="tpu_custom_call" | custom-call | tf_op jit(solution)/shard_map/root/pallas_call | solution.py:303
  3.3 17.2 %all_to_all.20 = f32[8,17,1,128]{3,2,1,0:T(1,128)S(1)} all-to-all(f32[8,17,1,128]{3,2,1,0:T(1,128)S(1)} %bitcast.20), channel_id=1, replica_groups={{56,48,40,32,24,16,8,0},{104,96,112,88,120,80,72,64},{57,49,41,33,25,17..., dimensions={0} | all-to-all | bytes 139264 | tf_op jit(solution)/shard_map/all_to_all | solution.py:278
  20.6 9.5 %all_to_all.21 = f32[8,25,1,128]{3,2,1,0:T(1,128)S(1)} all-to-all(f32[8,25,1,128]{3,2,1,0:T(1,128)S(1)} %bitcast.13), channel_id=1, replica_groups={{5,6,7,0,1,2,3,4},{13,14,15,8,9,10,11,12},{21,22,23,16,17,18,19,20},{29..., dimensions={0} | all-to-all | bytes 204800 | tf_op jit(solution)/shard_map/all_to_all | solution.py:278
  30.0 1.3 %middle.1 = (f32[32,64]{1,0:T(8,128)}, f32[136,128]{1,0:T(8,128)S(1)}, f32[8,128]{1,0:T(8,128)S(1)}) custom-call(f32[200,128]{1,0:T(8,128)S(1)} %bitcast.14, f32[4096,128]{1,0:T(8,128)S(1)} %get-tuple-element.10.prod_ref), custom_call_target="tpu_custom_call" | custom-call | tf_op jit(solution)/shard_map/middle/pallas_call | solution.py:321
  31.3 16.4 %all_to_all.22 = f32[8,17,1,128]{3,2,1,0:T(1,128)S(1)} all-to-all(f32[8,17,1,128]{3,2,1,0:T(1,128)S(1)} %bitcast.19), channel_id=1, replica_groups={{320,256,384,128,0,448,192,64},{321,257,385,129,1,449,193,65},{322,258,..., dimensions={0} | all-to-all | bytes 139264 | tf_op jit(solution)/shard_map/all_to_all | solution.py:278
  47.8 8.3 %all_to_all.23 = f32[8,17,1,128]{3,2,1,0:T(1,128)S(1)} all-to-all(f32[8,17,1,128]{3,2,1,0:T(1,128)S(1)} %bitcast.18), channel_id=1, replica_groups={{5,6,7,0,1,2,3,4},{13,14,15,8,9,10,11,12},{21,22,23,16,17,18,19,20},{29..., dimensions={0} | all-to-all | bytes 139264 | tf_op jit(solution)/shard_map/all_to_all | solution.py:278
  56.1 1.3 %last.1 = f32[32,64]{1,0:T(8,128)} custom-call(f32[8,128]{1,0:T(8,128)S(1)} %get-tuple-element.12.rest_ref, f32[136,128]{1,0:T(8,128)S(1)} %bitcast.16), custom_call_target="tpu_custom_call" | custom-call | tf_op jit(solution)/shard_map/last/pallas_call | solution.py:337
  (2 shorter events, 0.0 us)

commit v9 on v8

--- a/solution.py
+++ b/solution.py
@@ -243,7 +243,7 @@
         return acc + prod_ref[pl.ds(at, rows), :] * nx_ref[pl.ds(i, 1), :]
 
     acc_ref[...] = lax.fori_loop(
-        0, half, step, jnp.zeros((rows, 2 * wide), jnp.float32), unroll=8
+        0, half, step, jnp.zeros((rows, 2 * wide), jnp.float32), unroll=16
     )
     part = iota((second, 2 * wide), 1) // rank % fourth
     picked = acc_ref[pl.ds(0, second, stride=fourth), :]
@@ -296,7 +296,7 @@
     rank = factor_two.shape[1]
     wide = 2 * fourth * rank
     rows = first * second * fourth
-    chunks = 8
+    chunks = 4
     narrow = ((SLOTS * (PACK + 1), LANES), VMEM)
     full = ((SLOTS * (PACK + SUB + 1), LANES), VMEM)
     gram = ((SUB, LANES), VMEM)

time: 57.6 us -> 57.6 us (level)
  no operation moved by 1% of the time
where the time goes in v9:
time: 57.6 us; the launch traced here: 57.3 us
  blocking collectives  51.4 us (89%)
  Pallas kernels  5.23 us (9%)
  between operations  0.66 us (1%)
    all_to_all x4, blocking collectives, exchanged(): lax.all_to_all(parts, axes, 0, 0, tiled=True, axis_index_groups=groups)  51.4 us
    pallas_call x1, Pallas kernels, per_device(): call(functools.partial(root_kernel, first, chunks), 'root', (((rows // 2,...  2.65 us
    pallas_call x1, Pallas kernels, per_device(): call(functools.partial(middle_kernel, first, second, fourth), 'middle', (...  1.28 us
    pallas_call x1, Pallas kernels, per_device(): call(functools.partial(last_kernel, second), 'last', (((rank, second), VM...  1.27 us

profile of v9, /device:TPU:1, one launch (start us, length us, event | category | flops | bytes accessed | tf_op | source)
XLA Modules:
  0.0 57.3 jit_solution(304479927562613915)
XLA Ops:
  0.6 2.7 %root.1 = (f32[4096,128]{1,0:T(8,128)S(1)}, f32[136,128]{1,0:T(8,128)S(1)}, f32[8,128]{1,0:T(8,128)S(1)}) custom-call(bf16[8192,128]{1,0:T(8,128)(2,1)} %bitcast.21, f32[32,64]{1,0:T(8,128)} %bitcast.22, f32[32,128]{1,0:T(8,128)} %bitcast.23, f32[2,32]{1,0:T(2,128)} %f4_hbm.1), custom_call_target="tpu_custom_call" | custom-call | tf_op jit(solution)/shard_map/root/pallas_call | solution.py:303
  3.3 17.2 %all_to_all.20 = f32[8,17,1,128]{3,2,1,0:T(1,128)S(1)} all-to-all(f32[8,17,1,128]{3,2,1,0:T(1,128)S(1)} %bitcast.20), channel_id=1, replica_groups={{56,48,40,32,24,16,8,0},{104,96,112,88,120,80,72,64},{57,49,41,33,25,17..., dimensions={0} | all-to-all | bytes 139264 | tf_op jit(solution)/shard_map/all_to_all | solution.py:278
  20.5 9.4 %all_to_all.21 = f32[8,25,1,128]{3,2,1,0:T(1,128)S(1)} all-to-all(f32[8,25,1,128]{3,2,1,0:T(1,128)S(1)} %bitcast.13), channel_id=1, replica_groups={{5,6,7,0,1,2,3,4},{13,14,15,8,9,10,11,12},{21,22,23,16,17,18,19,20},{29..., dimensions={0} | all-to-all | bytes 204800 | tf_op jit(solution)/shard_map/all_to_all | solution.py:278
  30.0 1.3 %middle.1 = (f32[32,64]{1,0:T(8,128)}, f32[136,128]{1,0:T(8,128)S(1)}, f32[8,128]{1,0:T(8,128)S(1)}) custom-call(f32[200,128]{1,0:T(8,128)S(1)} %bitcast.14, f32[4096,128]{1,0:T(8,128)S(1)} %get-tuple-element.10.prod_ref), custom_call_target="tpu_custom_call" | custom-call | tf_op jit(solution)/shard_map/middle/pallas_call | solution.py:321
  31.3 16.4 %all_to_all.22 = f32[8,17,1,128]{3,2,1,0:T(1,128)S(1)} all-to-all(f32[8,17,1,128]{3,2,1,0:T(1,128)S(1)} %bitcast.19), channel_id=1, replica_groups={{320,256,384,128,0,448,192,64},{321,257,385,129,1,449,193,65},{322,258,..., dimensions={0} | all-to-all | bytes 139264 | tf_op jit(solution)/shard_map/all_to_all | solution.py:278
  47.7 8.3 %all_to_all.23 = f32[8,17,1,128]{3,2,1,0:T(1,128)S(1)} all-to-all(f32[8,17,1,128]{3,2,1,0:T(1,128)S(1)} %bitcast.18), channel_id=1, replica_groups={{5,6,7,0,1,2,3,4},{13,14,15,8,9,10,11,12},{21,22,23,16,17,18,19,20},{29..., dimensions={0} | all-to-all | bytes 139264 | tf_op jit(solution)/shard_map/all_to_all | solution.py:278
  56.0 1.3 %last.1 = f32[32,64]{1,0:T(8,128)} custom-call(f32[8,128]{1,0:T(8,128)S(1)} %get-tuple-element.12.rest_ref, f32[136,128]{1,0:T(8,128)S(1)} %bitcast.16), custom_call_target="tpu_custom_call" | custom-call | tf_op jit(solution)/shard_map/last/pallas_call | solution.py:337
  (2 shorter events, 0.0 us)
